TPU v7x, 256 devices: a whole 4x4x8 slice. The times are simulated.
256 devices in a mesh: gx: 4 (over y), gy: 8 (over z_hi, core), gz: 8 (over z_lo, x).
Axes of the slice: x: 4, y: 4, z: 8 (z_hi: 4, z_lo: 2; z = z_hi * 2 + z_lo), core: 2. Of those that a mesh axis runs over, the one named last changes fastest.
Arguments:
- states: float32 [41, 32, 128, 1024], P(None, 'gz', 'gy', 'gx'), may hold values from 0 to 1
- prior_states: float32 [41, 32, 128, 1024], P(None, 'gz', 'gy', 'gx'), may hold values from 0 to 1
- cell_layers: int32 [32, 128, 1024], P('gz', 'gy', 'gx'), may hold values from 0 to 2
- fiber_classes: int32 [32, 128, 1024], P('gz', 'gy', 'gx'), may hold values from 0 to 15
- writer_stripe: int32 [64], replicated, may hold values from 0 to 63, each once
- gate_half: float32 [3, 40], replicated, may hold values from -1 to 1.5
- gate_slope: float32 [3, 40], replicated, may hold values from 1 to 8
- gate_tau: float32 [3, 40], replicated, may hold values from 1 to 40
- gate_conduct: float32 [3, 40], replicated, may hold values from 0.002 to 0.025
- gate_reversal: float32 [3, 40], replicated, may hold values from -1.5 to 1.5
- fiber_conduct: float32 [16, 3], replicated, may hold values from 0.02 to 0.15
Outputs:
- new_states: float32 [41, 32, 128, 1024], P(None, 'gz', 'gy', 'gx')
- stripes: float32 [41, 4096, 1, 1024], P(None, ('gy', 'gz'), None, 'gx')
Inputs may be any that keep to these rules, and one draw needn't show every extreme that they name: `writer_stripe`: every one of the 64 stripes has exactly one writer.
All inputs are finite; a program needn't handle non-finite values.
Results may differ from a plain program's by a relative error of at most 0.000062.
Values sent between devices are 32-bit elements; how exact they have to be, the bound alone decides.
A program may use at most 64 MiB of HBM per device.

v0:
```python
import jax
import jax.numpy as jnp
from jax import lax
from jax.sharding import PartitionSpec as P

STEPS = 4


def in_blocks(value, dim, devices):
    before, after = (value.shape[:dim], value.shape[dim + 1 :])
    return jnp.moveaxis(value.reshape(*before, devices, -1, *after), dim, 0)


def cut_rows(length, count):
    step = length // count
    if step >= 8:
        step -= step % 8
    return [step * k for k in range(1, count)]


def joined_along(parts, dim):
    parts = jnp.moveaxis(parts, 0, dim)
    dims = parts.shape
    return parts.reshape(*dims[:dim], dims[dim] * dims[dim + 1], *dims[dim + 2 :])


def cut_exchange(value, axis, pieces, split_dim, concat_dim):
    parts = in_blocks(value, split_dim, lax.axis_size(axis))
    widest = max(range(1, max(2, parts.ndim - 1)), key=lambda d: parts.shape[d])
    finished = []
    for share in jnp.split(parts, cut_rows(parts.shape[widest], pieces), axis=widest):
        if share.size:
            finished.append(lax.all_to_all(share, axis, split_axis=0, concat_axis=0, tiled=True))
    return joined_along(jnp.concatenate(finished, axis=widest), concat_dim)


def extended(value, sides, width):
    edges = {}
    for axis, dim in sides:
        devices, length = (lax.axis_size(axis), value.shape[dim])
        up = [(i, (i + 1) % devices) for i in range(devices - 1)]
        last = lax.slice_in_dim(value, length - width, length, axis=dim)
        first = lax.slice_in_dim(value, 0, width, axis=dim)
        edges[dim] = (
            lax.ppermute(last, axis, up),
            lax.ppermute(first, axis, [(b, a) for a, b in up]),
        )
    done = []
    for _, dim in sides:
        low, high = edges[dim]
        around = [(width, width) if d in done else (0, 0) for d in range(value.ndim)]
        value = jnp.concatenate([jnp.pad(low, around), value, jnp.pad(high, around)], axis=dim)
        done.append(dim)
    return value


def pick_layers(cell_layers, params):
    tail_shape = (1,) * cell_layers.ndim
    layer_count = params.shape[0]
    picked = jnp.broadcast_to(
        params[layer_count - 1].reshape((-1,) + tail_shape), (params.shape[1],) + cell_layers.shape
    )
    for which_layer in range(layer_count - 2, -1, -1):
        picked = jnp.where(
            cell_layers[None] == which_layer,
            params[which_layer].reshape((-1,) + tail_shape),
            picked,
        )
    return picked


def edge_masks(device_index, device_count, length, dim):
    position = device_index * length + jnp.arange(length, dtype=jnp.int32)
    extent = length * device_count
    view_shape = [1, 1, 1]
    view_shape[dim] = length
    below_ok = (position > 0).astype(jnp.float32).reshape(view_shape)
    above_ok = (position < extent - 1).astype(jnp.float32).reshape(view_shape)
    return (below_ok, above_ok)


def per_device(
    states,
    prior_states,
    cell_layers,
    fiber_classes,
    writer_stripe,
    gate_half,
    gate_slope,
    gate_tau,
    gate_conduct,
    gate_reversal,
    fiber_conduct,
):
    states_count = prior_states.shape[0]
    writers = lax.axis_size("gy") * lax.axis_size("gz")
    pieces = prior_states.reshape(states_count, writers, -1, prior_states.shape[3])
    outgoing = jnp.take(pieces, writer_stripe, axis=1)
    stripes = cut_exchange(outgoing, ("gy", "gz"), 2, 1, 1)
    cells_t, cells_w, cells_d = (states.shape[1], states.shape[2], states.shape[3])
    fibers = fiber_conduct.shape[0]
    onehot = (
        fiber_classes[None] == jnp.arange(fibers, dtype=jnp.int32)[:, None, None, None]
    ).astype(jnp.float32)
    sigma_cells = jnp.dot(
        fiber_conduct.T, onehot.reshape(fibers, -1), precision=lax.Precision.HIGHEST
    )
    sigma_cells = sigma_cells.reshape(3, cells_t, cells_w, cells_d)
    half_cells = pick_layers(cell_layers, gate_half)
    slope_cells = pick_layers(cell_layers, gate_slope)
    tau_cells = pick_layers(cell_layers, gate_tau)
    cond_cells = pick_layers(cell_layers, gate_conduct)
    rev_cells = pick_layers(cell_layers, gate_reversal)
    below_t, above_t = edge_masks(lax.axis_index("gz"), lax.axis_size("gz"), cells_t, 0)
    below_w, above_w = edge_masks(lax.axis_index("gy"), lax.axis_size("gy"), cells_w, 1)
    below_d, above_d = edge_masks(lax.axis_index("gx"), lax.axis_size("gx"), cells_d, 2)
    voltage = states[0]
    gate_states = states[1:]
    for step_index in range(STEPS):
        steady = jax.nn.sigmoid((voltage[None] - half_cells) * slope_cells)
        decay_rate = jnp.exp(-1.0 / (tau_cells * (1.0 + steady)))
        gate_states = steady + (gate_states - steady) * decay_rate
        current = jnp.sum(cond_cells * gate_states * (voltage[None] - rev_cells), axis=0)
        excited = voltage - current
        padded = extended(excited, (("gx", 2), ("gy", 1), ("gz", 0)), 1)
        across = above_t * (padded[2:, 1:-1, 1:-1] - excited) + below_t * (
            padded[:-2, 1:-1, 1:-1] - excited
        )
        widthwise = above_w * (padded[1:-1, 2:, 1:-1] - excited) + below_w * (
            padded[1:-1, :-2, 1:-1] - excited
        )
        depthwise = above_d * (padded[1:-1, 1:-1, 2:] - excited) + below_d * (
            padded[1:-1, 1:-1, :-2] - excited
        )
        voltage = (
            excited
            + sigma_cells[0] * across
            + sigma_cells[1] * widthwise
            + sigma_cells[2] * depthwise
        )
    new_states = jnp.concatenate([voltage[None], gate_states], axis=0)
    return (new_states, stripes)


def solution(mesh):
    in_specs = (
        P(None, "gz", "gy", "gx"),
        P(None, "gz", "gy", "gx"),
        P("gz", "gy", "gx"),
        P("gz", "gy", "gx"),
        P(),
        P(),
        P(),
        P(),
        P(),
        P(),
        P(),
    )
    out_specs = (P(None, "gz", "gy", "gx"), P(None, ("gy", "gz"), None, "gx"))
    return jax.shard_map(
        per_device, mesh=mesh, in_specs=in_specs, out_specs=out_specs, check_vma=False
    )
```

profile of v0, /device:TPU:95, one launch (start us, length us, event | category | flops | bytes accessed | tf_op | source)
XLA Modules:
  0.0 175.1 jit_solution(8179882716352205049)
XLA Ops:
  0.6 0.8 slice_bitcast_fusion.16
  1.5 0.9 broadcast_compare_fusion.1
  2.3 0.8 slice_bitcast_fusion.1
  3.2 0.8 slice_bitcast_fusion.10
  4.0 0.8 slice_bitcast_fusion.4
  4.9 6.7 %multiply_reduce_fusion.3 = (f32[4,16,256]{2,1,0:T(8,128)S(1)}, f32[40,4,16,256]{3,2,1,0:T(8,128)}) fusion(f32[40]{0:T(128)S(1)} %get-tuple-element.58, f32[40]{0:T(128)S(1)} %get-tuple-element.59, f32[40]{0:T(128)S(1)} %get-tuple-element.57, f32[4,16,256]{2,1,0:T(8,128)S(1)} %slice_bitcast_fusion.1, f32[40]{0:T(128)S(1)} %get-tuple-element.55, ...), kind=kLoop, calls=%fused_computation.12 | loop fusion | flops 16367616 | bytes 5409120 | tf_op jit(solution)/shard_map/reduce_sum | solution.py:123
  11.7 0.9 fusion.95
  12.5 0.6 fusion.106
  13.1 2.6 %collective-permute-start.3 = (f32[4,1,256]{2,1,0:T(1,128)}, f32[4,1,256]{2,1,0:T(1,128)}, u32[]{:S(2)}, u32[]{:S(2)}) collective-permute-start(f32[4,1,256]{2,1,0:T(1,128)} %get-tuple-element.39), channel_id=1, source_target_pairs={{8,0},{16,8},{24,16},{32,24},{40,32},{48,40},{56,48},{9,1},{17,9},... | collective-permute-start | bytes 12296 | tf_op jit(solution)/shard_map/ppermute | solution.py:46
  15.7 6.0 %collective-permute-start = (f32[4,1,256]{2,1,0:T(1,128)}, f32[4,1,256]{2,1,0:T(1,128)}, u32[]{:S(2)}, u32[]{:S(2)}) collective-permute-start(f32[4,1,256]{2,1,0:T(1,128)} %get-tuple-element.40), channel_id=1, source_target_pairs={{0,8},{8,16},{16,24},{24,32},{32,40},{40,48},{48,56},{1,9},{9,17},... | collective-permute-start | bytes 12296 | tf_op jit(solution)/shard_map/ppermute | solution.py:45
  21.7 0.6 fusion.105
  22.3 2.4 %collective-permute-start.4 = (f32[1,16,256]{2,1,0:T(8,128)}, f32[1,16,256]{2,1,0:T(8,128)}, u32[]{:S(2)}, u32[]{:S(2)}) collective-permute-start(f32[1,16,256]{2,1,0:T(8,128)} %get-tuple-element.37), channel_id=1, source_target_pairs={{1,0},{2,1},{3,2},{4,3},{5,4},{6,5},{7,6},{9,8},{10,9},{11,10},{12... | collective-permute-start | bytes 49160 | tf_op jit(solution)/shard_map/ppermute | solution.py:46
  24.8 4.9 %collective-permute-start.5 = (f32[1,16,256]{2,1,0:T(8,128)}, f32[1,16,256]{2,1,0:T(8,128)}, u32[]{:S(2)}, u32[]{:S(2)}) collective-permute-start(f32[1,16,256]{2,1,0:T(8,128)} %get-tuple-element.38), channel_id=1, source_target_pairs={{0,1},{1,2},{2,3},{3,4},{4,5},{5,6},{6,7},{8,9},{9,10},{10,11},{11... | collective-permute-start | bytes 49160 | tf_op jit(solution)/shard_map/ppermute | solution.py:45
  29.8 2.4 %collective-permute-start.2 = (f32[4,16,1]{2,1,0:T(8,128)S(1)}, f32[4,16,1]{2,1,0:T(8,128)S(1)}, u32[]{:S(2)}, u32[]{:S(2)}) collective-permute-start(f32[4,16,1]{2,1,0:T(8,128)S(1)} %get-tuple-element.41), channel_id=1, source_target_pairs={{64,0},{128,64},{192,128},{65,1},{129,65},{193,129},{66,2},{130,66... | collective-permute-start | bytes 776 | tf_op jit(solution)/shard_map/ppermute | solution.py:46
  32.2 1.6 copy.20
  33.8 2.4 %gather_fusion = f32[64,41,256]{2,1,0:T(8,128)} fusion(f32[41,64,256]{2,0,1:T(8,128)S(1)} %bitcast.56, s32[1024]{0:T(1024)S(1)} %pad_clamp_fusion), kind=kCustom, calls=%fused_computation | custom fusion | bytes 5374208 | tf_op jit(solution)/shard_map/jit(_take)/gather | solution.py:98
  36.2 2.2 %fusion = f32[64,41,1,1,256]{4,1,0,3,2:T(8,128)S(1)} fusion(f32[64,41,256]{2,1,0:T(8,128)} %gather_fusion, pred[64]{0:T(512)(128)(4,1)S(1)} %compare_and_fusion), kind=kLoop, calls=%fused_computation.3 | loop fusion | flops 671744 | bytes 5374016 | tf_op jit(solution)/shard_map/transpose | solution.py:11
  38.4 1.0 slice_bitcast_fusion
  39.4 8.6 %all-to-all-start = ((f32[64,16,1,1,256]{4,1,3,2,0:T(8,128)}), f32[64,16,1,1,256]{4,1,3,2,0:T(8,128)}, u32[]{:S(2)}, u32[]{:S(2)}) async-start(f32[64,16,1,1,256]{4,1,3,2,0:T(8,128)} %slice_bitcast_fusion), calls=%async_computation | async-start | bytes 2097152 | tf_op jit(solution)/shard_map/all_to_all | solution.py:33
  48.1 0.6 compare_convert_fusion.4
  48.7 0.4 convolution_bitcast_fusion
  49.2 0.5 slice_reduce_fusion.2
  49.7 0.6 compare_convert_fusion.2
  50.4 1.3 collective-permute-start.1
  51.7 0.8 pad.51
  52.4 0.8 pad.50
  53.2 2.2 %collective-permute-done.1 = f32[4,16,1]{2,1,0:T(8,128)S(1)} collective-permute-done((f32[4,16,1]{2,1,0:T(8,128)S(1)}, f32[4,16,1]{2,1,0:T(8,128)S(1)}, u32[]{:S(2)}, u32[]{:S(2)}) %collective-permute-start.1) | collective-permute-done | bytes 288 | tf_op jit(solution)/shard_map/ppermute | solution.py:45
  55.4 0.9 fusion.76
  56.4 5.9 %multiply_reduce_fusion.2 = (f32[4,16,256]{2,1,0:T(8,128)S(1)}, f32[40,4,16,256]{3,2,1,0:T(8,128)S(1)}) fusion(f32[4,16,256]{2,1,0:T(8,128)S(1)} %fusion.76, f32[40]{0:T(128)} %copy-done.16, f32[40]{0:T(128)} %copy-done.18, f32[40]{0:T(128)} %copy-done.14, f32[40]{0:T(128)} %copy-done.28, f32[40]{0:T(128)} %copy-done.30, f32[40]{0:T(128)} %copy-done.26, ...), kind=kLoop, calls=%fused_computation.10 | loop fusion | flops 16367616 | bytes 5409120 | tf_op jit(solution)/shard_map/reduce_sum | solution.py:123
  62.3 3.0 %collective-permute-start.9 = (f32[4,1,256]{2,1,0:T(1,128)S(1)}, f32[4,1,256]{2,1,0:T(1,128)S(1)}, u32[]{:S(2)}, u32[]{:S(2)}) collective-permute-start(f32[4,1,256]{2,1,0:T(1,128)S(1)} %get-tuple-element.33), channel_id=1, source_target_pairs={{8,0},{16,8},{24,16},{32,24},{40,32},{48,40},{56,48},{9,1},{17,9},... | collective-permute-start | bytes 12296 | tf_op jit(solution)/shard_map/ppermute | solution.py:46
  65.3 5.2 %collective-permute-start.6 = (f32[4,1,256]{2,1,0:T(1,128)S(1)}, f32[4,1,256]{2,1,0:T(1,128)S(1)}, u32[]{:S(2)}, u32[]{:S(2)}) collective-permute-start(f32[4,1,256]{2,1,0:T(1,128)S(1)} %get-tuple-element.34), channel_id=1, source_target_pairs={{0,8},{8,16},{16,24},{24,32},{32,40},{40,48},{48,56},{1,9},{9,17},... | collective-permute-start | bytes 12296 | tf_op jit(solution)/shard_map/ppermute | solution.py:45
  70.6 2.5 %collective-permute-start.10 = (f32[1,16,256]{2,1,0:T(8,128)S(1)}, f32[1,16,256]{2,1,0:T(8,128)S(1)}, u32[]{:S(2)}, u32[]{:S(2)}) collective-permute-start(f32[1,16,256]{2,1,0:T(8,128)S(1)} %get-tuple-element.31), channel_id=1, source_target_pairs={{1,0},{2,1},{3,2},{4,3},{5,4},{6,5},{7,6},{9,8},{10,9},{11,10},{12... | collective-permute-start | bytes 49160 | tf_op jit(solution)/shard_map/ppermute | solution.py:46
  73.1 4.9 %collective-permute-start.11 = (f32[1,16,256]{2,1,0:T(8,128)S(1)}, f32[1,16,256]{2,1,0:T(8,128)S(1)}, u32[]{:S(2)}, u32[]{:S(2)}) collective-permute-start(f32[1,16,256]{2,1,0:T(8,128)S(1)} %get-tuple-element.32), channel_id=1, source_target_pairs={{0,1},{1,2},{2,3},{3,4},{4,5},{5,6},{6,7},{8,9},{9,10},{10,11},{11... | collective-permute-start | bytes 49160 | tf_op jit(solution)/shard_map/ppermute | solution.py:45
  78.1 2.1 %collective-permute-start.8 = (f32[4,16,1]{2,1,0:T(8,128)S(1)}, f32[4,16,1]{2,1,0:T(8,128)S(1)}, u32[]{:S(2)}, u32[]{:S(2)}) collective-permute-start(f32[4,16,1]{2,1,0:T(8,128)S(1)} %get-tuple-element.35), channel_id=1, source_target_pairs={{64,0},{128,64},{192,128},{65,1},{129,65},{193,129},{66,2},{130,66... | collective-permute-start | bytes 776 | tf_op jit(solution)/shard_map/ppermute | solution.py:46
  80.1 1.3 collective-permute-start.7
  81.5 2.8 %copy.22 = f32[64,25,1,1,256]{4,3,2,1,0:T(1,128)} copy(f32[64,25,1,1,256]{4,1,0,3,2:T(8,128)S(1)} %slice-done) | data formatting | bytes 3276800 | tf_op jit(solution)/shard_map/split | solution.py:31
  84.6 0.2 collective-permute-done.7
  84.8 0.2 fusion.53
  85.1 9.1 %all-to-all-start.1 = ((f32[64,25,1,1,256]{4,3,2,1,0:T(1,128)}), f32[64,25,1,1,256]{4,3,2,1,0:T(1,128)}, u32[]{:S(2)}, u32[]{:S(2)}) async-start(f32[64,25,1,1,256]{4,3,2,1,0:T(1,128)} %copy.22), calls=%async_computation.1 | async-start | bytes 3276800 | tf_op jit(solution)/shard_map/all_to_all | solution.py:33
  94.3 4.2 %multiply_reduce_fusion.1 = (f32[4,16,256]{2,1,0:T(8,128)S(1)}, f32[40,4,16,256]{3,2,1,0:T(8,128)S(1)}) fusion(f32[4,16,256]{2,1,0:T(8,128)S(1)} %fusion.53, f32[40]{0:T(128)S(1)} %copy-done.17, f32[40]{0:T(128)S(1)} %copy-done.19, f32[40]{0:T(128)S(1)} %copy-done.15, f32[40]{0:T(128)S(1)} %copy-done.29, f32[40]{0:T(128)S(1)} %copy-done.31, ...), kind=kLoop, calls=%fused_computation.8 | loop fusion | flops 16367616 | bytes 5409120 | tf_op jit(solution)/shard_map/reduce_sum | solution.py:123
  98.5 2.2 %collective-permute-start.15 = (f32[4,1,256]{2,1,0:T(1,128)S(1)}, f32[4,1,256]{2,1,0:T(1,128)S(1)}, u32[]{:S(2)}, u32[]{:S(2)}) collective-permute-start(f32[4,1,256]{2,1,0:T(1,128)S(1)} %get-tuple-element.27), channel_id=1, source_target_pairs={{8,0},{16,8},{24,16},{32,24},{40,32},{48,40},{56,48},{9,1},{17,9},... | collective-permute-start | bytes 12296 | tf_op jit(solution)/shard_map/ppermute | solution.py:46
  100.8 5.4 %collective-permute-start.12 = (f32[4,1,256]{2,1,0:T(1,128)S(1)}, f32[4,1,256]{2,1,0:T(1,128)S(1)}, u32[]{:S(2)}, u32[]{:S(2)}) collective-permute-start(f32[4,1,256]{2,1,0:T(1,128)S(1)} %get-tuple-element.28), channel_id=1, source_target_pairs={{0,8},{8,16},{16,24},{24,32},{32,40},{40,48},{48,56},{1,9},{9,17},... | collective-permute-start | bytes 12296 | tf_op jit(solution)/shard_map/ppermute | solution.py:45
  106.2 2.5 %collective-permute-start.16 = (f32[1,16,256]{2,1,0:T(8,128)S(1)}, f32[1,16,256]{2,1,0:T(8,128)S(1)}, u32[]{:S(2)}, u32[]{:S(2)}) collective-permute-start(f32[1,16,256]{2,1,0:T(8,128)S(1)} %get-tuple-element.25), channel_id=1, source_target_pairs={{1,0},{2,1},{3,2},{4,3},{5,4},{6,5},{7,6},{9,8},{10,9},{11,10},{12... | collective-permute-start | bytes 49160 | tf_op jit(solution)/shard_map/ppermute | solution.py:46
  108.7 4.9 %collective-permute-start.17 = (f32[1,16,256]{2,1,0:T(8,128)S(1)}, f32[1,16,256]{2,1,0:T(8,128)S(1)}, u32[]{:S(2)}, u32[]{:S(2)}) collective-permute-start(f32[1,16,256]{2,1,0:T(8,128)S(1)} %get-tuple-element.26), channel_id=1, source_target_pairs={{0,1},{1,2},{2,3},{3,4},{4,5},{5,6},{6,7},{8,9},{9,10},{10,11},{11... | collective-permute-start | bytes 49160 | tf_op jit(solution)/shard_map/ppermute | solution.py:45
  113.7 2.9 %collective-permute-start.14 = (f32[4,16,1]{2,1,0:T(8,128)S(1)}, f32[4,16,1]{2,1,0:T(8,128)S(1)}, u32[]{:S(2)}, u32[]{:S(2)}) collective-permute-start(f32[4,16,1]{2,1,0:T(8,128)S(1)} %get-tuple-element.29), channel_id=1, source_target_pairs={{64,0},{128,64},{192,128},{65,1},{129,65},{193,129},{66,2},{130,66... | collective-permute-start | bytes 776 | tf_op jit(solution)/shard_map/ppermute | solution.py:46
  116.6 16.7 %collective-permute-done.15 = f32[4,1,256]{2,1,0:T(1,128)S(1)} collective-permute-done((f32[4,1,256]{2,1,0:T(1,128)S(1)}, f32[4,1,256]{2,1,0:T(1,128)S(1)}, u32[]{:S(2)}, u32[]{:S(2)}) %collective-permute-start.15) | collective-permute-done | bytes 4128 | tf_op jit(solution)/shard_map/ppermute | solution.py:46
  133.3 1.3 collective-permute-start.13
  134.6 0.1 pad.58
  134.7 3.2 %collective-permute-done.13 = f32[4,16,1]{2,1,0:T(8,128)S(1)} collective-permute-done((f32[4,16,1]{2,1,0:T(8,128)S(1)}, f32[4,16,1]{2,1,0:T(8,128)S(1)}, u32[]{:S(2)}, u32[]{:S(2)}) %collective-permute-start.13) | collective-permute-done | bytes 288 | tf_op jit(solution)/shard_map/ppermute | solution.py:45
  137.9 0.2 fusion.30
  138.1 4.2 %multiply_reduce_fusion = (f32[4,16,256]{2,1,0:T(8,128)S(1)}, f32[40,4,16,256]{3,2,1,0:T(8,128)S(1)}) fusion(f32[4,16,256]{2,1,0:T(8,128)S(1)} %fusion.30, f32[40]{0:T(128)S(1)} %copy-done.17, f32[40]{0:T(128)S(1)} %copy-done.19, f32[40]{0:T(128)S(1)} %copy-done.15, f32[40]{0:T(128)S(1)} %copy-done.29, f32[40]{0:T(128)S(1)} %copy-done.31, ...), kind=kLoop, calls=%fused_computation.6 | loop fusion | flops 16367616 | bytes 5409120 | tf_op jit(solution)/shard_map/reduce_sum | solution.py:123
  142.3 1.9 %collective-permute-start.21 = (f32[4,1,256]{2,1,0:T(1,128)S(1)}, f32[4,1,256]{2,1,0:T(1,128)S(1)}, u32[]{:S(2)}, u32[]{:S(2)}) collective-permute-start(f32[4,1,256]{2,1,0:T(1,128)S(1)} %get-tuple-element.21), channel_id=1, source_target_pairs={{8,0},{16,8},{24,16},{32,24},{40,32},{48,40},{56,48},{9,1},{17,9},... | collective-permute-start | bytes 12296 | tf_op jit(solution)/shard_map/ppermute | solution.py:46
  144.2 5.8 %collective-permute-start.18 = (f32[4,1,256]{2,1,0:T(1,128)S(1)}, f32[4,1,256]{2,1,0:T(1,128)S(1)}, u32[]{:S(2)}, u32[]{:S(2)}) collective-permute-start(f32[4,1,256]{2,1,0:T(1,128)S(1)} %get-tuple-element.22), channel_id=1, source_target_pairs={{0,8},{8,16},{16,24},{24,32},{32,40},{40,48},{48,56},{1,9},{9,17},... | collective-permute-start | bytes 12296 | tf_op jit(solution)/shard_map/ppermute | solution.py:45
  150.0 2.5 %collective-permute-start.22 = (f32[1,16,256]{2,1,0:T(8,128)S(1)}, f32[1,16,256]{2,1,0:T(8,128)S(1)}, u32[]{:S(2)}, u32[]{:S(2)}) collective-permute-start(f32[1,16,256]{2,1,0:T(8,128)S(1)} %get-tuple-element.19), channel_id=1, source_target_pairs={{1,0},{2,1},{3,2},{4,3},{5,4},{6,5},{7,6},{9,8},{10,9},{11,10},{12... | collective-permute-start | bytes 49160 | tf_op jit(solution)/shard_map/ppermute | solution.py:46
  152.5 4.9 %collective-permute-start.23 = (f32[1,16,256]{2,1,0:T(8,128)S(1)}, f32[1,16,256]{2,1,0:T(8,128)S(1)}, u32[]{:S(2)}, u32[]{:S(2)}) collective-permute-start(f32[1,16,256]{2,1,0:T(8,128)S(1)} %get-tuple-element.20), channel_id=1, source_target_pairs={{0,1},{1,2},{2,3},{3,4},{4,5},{5,6},{6,7},{8,9},{9,10},{10,11},{11... | collective-permute-start | bytes 49160 | tf_op jit(solution)/shard_map/ppermute | solution.py:45
  157.5 2.9 %collective-permute-start.20 = (f32[4,16,1]{2,1,0:T(8,128)S(1)}, f32[4,16,1]{2,1,0:T(8,128)S(1)}, u32[]{:S(2)}, u32[]{:S(2)}) collective-permute-start(f32[4,16,1]{2,1,0:T(8,128)S(1)} %get-tuple-element.23), channel_id=1, source_target_pairs={{64,0},{128,64},{192,128},{65,1},{129,65},{193,129},{66,2},{130,66... | collective-permute-start | bytes 776 | tf_op jit(solution)/shard_map/ppermute | solution.py:46
  160.4 1.3 collective-permute-start.19
  161.8 3.2 %collective-permute-done.19 = f32[4,16,1]{2,1,0:T(8,128)S(1)} collective-permute-done((f32[4,16,1]{2,1,0:T(8,128)S(1)}, f32[4,16,1]{2,1,0:T(8,128)S(1)}, u32[]{:S(2)}, u32[]{:S(2)}) %collective-permute-start.19) | collective-permute-done | bytes 288 | tf_op jit(solution)/shard_map/ppermute | solution.py:45
  165.1 0.2 fusion.7
  165.2 1.8 %pad_maximum_fusion = f32[41,4,16,256]{3,2,1,0:T(8,128)} fusion(f32[40,4,16,256]{3,2,1,0:T(8,128)S(1)} %get-tuple-element.12, f32[1,4,16,256]{3,2,1,0:T(8,128)S(1)} %fusion.7), kind=kLoop, calls=%fused_computation.4 | loop fusion | flops 671744 | bytes 5373952 | tf_op jit(solution)/shard_map/concatenate | solution.py:141
  167.1 1.8 %copy.23 = f32[64,16,1,1,256]{4,0,1,3,2:T(8,128)S(1)} copy(f32[64,16,1,1,256]{4,1,3,2,0:T(8,128)} %all-to-all-done) | data formatting | bytes 2097152 | tf_op jit(solution)/shard_map/all_to_all | solution.py:33
  168.9 1.6 copy.24
  170.5 0.3 maximum_bitcast_fusion
  170.8 4.3 %copy.25 = f32[41,64,1,256]{3,2,1,0:T(1,128)} copy(f32[41,64,1,256]{3,1,0,2:T(8,128)S(1)} %maximum_bitcast_fusion) | data formatting | bytes 5373952
  (123 shorter events, 1.1 us)
Async XLA Ops:
  0.6 48.1 %copy-start = (f32[16,3]{0,1:T(4,128)S(1)}, f32[16,3]{0,1:T(4,128)}, u32[]{:S(2)}) copy-start(f32[16,3]{0,1:T(4,128)} %param.21) | copy-start | bytes 580
  1.4 10.1 %copy-start.26 = (f32[40]{0:T(128)}, f32[40]{0:T(128)S(1)}, u32[]{:S(2)}) copy-start(f32[40]{0:T(128)S(1)} %get-tuple-element.54) | copy-start | bytes 484
  1.4 10.1 %copy-start.28 = (f32[40]{0:T(128)}, f32[40]{0:T(128)S(1)}, u32[]{:S(2)}) copy-start(f32[40]{0:T(128)S(1)} %get-tuple-element.55) | copy-start | bytes 484
  1.4 10.1 %copy-start.30 = (f32[40]{0:T(128)}, f32[40]{0:T(128)S(1)}, u32[]{:S(2)}) copy-start(f32[40]{0:T(128)S(1)} %get-tuple-element.56) | copy-start | bytes 484
  4.0 7.6 %copy-start.4 = (f32[40]{0:T(128)}, f32[40]{0:T(128)S(1)}, u32[]{:S(2)}) copy-start(f32[40]{0:T(128)S(1)} %get-tuple-element.49) | copy-start | bytes 484
  4.0 7.6 %copy-start.6 = (f32[40]{0:T(128)}, f32[40]{0:T(128)S(1)}, u32[]{:S(2)}) copy-start(f32[40]{0:T(128)S(1)} %get-tuple-element.50) | copy-start | bytes 484
  4.0 7.6 %copy-start.8 = (f32[40]{0:T(128)}, f32[40]{0:T(128)S(1)}, u32[]{:S(2)}) copy-start(f32[40]{0:T(128)S(1)} %get-tuple-element.63) | copy-start | bytes 484
  4.0 7.6 %copy-start.10 = (f32[40]{0:T(128)}, f32[40]{0:T(128)S(1)}, u32[]{:S(2)}) copy-start(f32[40]{0:T(128)S(1)} %get-tuple-element.64) | copy-start | bytes 484
  4.0 7.6 %copy-start.12 = (f32[40]{0:T(128)}, f32[40]{0:T(128)S(1)}, u32[]{:S(2)}) copy-start(f32[40]{0:T(128)S(1)} %get-tuple-element.65) | copy-start | bytes 484
  4.8 6.8 %copy-start.14 = (f32[40]{0:T(128)}, f32[40]{0:T(128)S(1)}, u32[]{:S(2)}) copy-start(f32[40]{0:T(128)S(1)} %get-tuple-element.57) | copy-start | bytes 484
  4.8 6.8 %copy-start.16 = (f32[40]{0:T(128)}, f32[40]{0:T(128)S(1)}, u32[]{:S(2)}) copy-start(f32[40]{0:T(128)S(1)} %get-tuple-element.58) | copy-start | bytes 484
  4.8 6.8 %copy-start.18 = (f32[40]{0:T(128)}, f32[40]{0:T(128)S(1)}, u32[]{:S(2)}) copy-start(f32[40]{0:T(128)S(1)} %get-tuple-element.59) | copy-start | bytes 484
  4.8 6.8 %copy-start.20 = (f32[40]{0:T(128)}, f32[40]{0:T(128)S(1)}, u32[]{:S(2)}) copy-start(f32[40]{0:T(128)S(1)} %get-tuple-element.60) | copy-start | bytes 484
  4.8 6.8 %copy-start.22 = (f32[40]{0:T(128)}, f32[40]{0:T(128)S(1)}, u32[]{:S(2)}) copy-start(f32[40]{0:T(128)S(1)} %get-tuple-element.61) | copy-start | bytes 484
  4.9 6.8 %copy-start.24 = (f32[40]{0:T(128)}, f32[40]{0:T(128)S(1)}, u32[]{:S(2)}) copy-start(f32[40]{0:T(128)S(1)} %get-tuple-element.62) | copy-start | bytes 484
  4.9 27.3 %copy-start.36 = (s32[64]{0:T(128)S(1)}, s32[64]{0:T(128)}, u32[]{:S(2)}) copy-start(s32[64]{0:T(128)} %param.15) | copy-start | bytes 772
  4.9 27.4 %copy-start.2 = (f32[41,4,16,256]{3,2,1,0:T(8,128)S(1)}, f32[41,4,16,256]{3,2,1,0:T(8,128)}, u32[]{:S(2)}) copy-start(f32[41,4,16,256]{3,2,1,0:T(8,128)} %param.12) | copy-start | bytes 8060932
  13.1 37.2 %collective-permute-start.3 = (f32[4,1,256]{2,1,0:T(1,128)}, f32[4,1,256]{2,1,0:T(1,128)}, u32[]{:S(2)}, u32[]{:S(2)}) collective-permute-start(f32[4,1,256]{2,1,0:T(1,128)} %get-tuple-element.39), channel_id=1, source_target_pairs={{8,0},{16,8},{24,16},{32,24},{40,32},{48,40},{56,48},{9,1},{17,9},... | collective-permute-start | bytes 12296 | tf_op jit(solution)/shard_map/ppermute | solution.py:46
  15.7 36.7 %collective-permute-start = (f32[4,1,256]{2,1,0:T(1,128)}, f32[4,1,256]{2,1,0:T(1,128)}, u32[]{:S(2)}, u32[]{:S(2)}) collective-permute-start(f32[4,1,256]{2,1,0:T(1,128)} %get-tuple-element.40), channel_id=1, source_target_pairs={{0,8},{8,16},{16,24},{24,32},{32,40},{40,48},{48,56},{1,9},{9,17},... | collective-permute-start | bytes 12296 | tf_op jit(solution)/shard_map/ppermute | solution.py:45
  22.3 33.1 %collective-permute-start.4 = (f32[1,16,256]{2,1,0:T(8,128)}, f32[1,16,256]{2,1,0:T(8,128)}, u32[]{:S(2)}, u32[]{:S(2)}) collective-permute-start(f32[1,16,256]{2,1,0:T(8,128)} %get-tuple-element.37), channel_id=1, source_target_pairs={{1,0},{2,1},{3,2},{4,3},{5,4},{6,5},{7,6},{9,8},{10,9},{11,10},{12... | collective-permute-start | bytes 49160 | tf_op jit(solution)/shard_map/ppermute | solution.py:46
  24.8 30.6 %collective-permute-start.5 = (f32[1,16,256]{2,1,0:T(8,128)}, f32[1,16,256]{2,1,0:T(8,128)}, u32[]{:S(2)}, u32[]{:S(2)}) collective-permute-start(f32[1,16,256]{2,1,0:T(8,128)} %get-tuple-element.38), channel_id=1, source_target_pairs={{0,1},{1,2},{2,3},{3,4},{4,5},{5,6},{6,7},{8,9},{9,10},{10,11},{11... | collective-permute-start | bytes 49160 | tf_op jit(solution)/shard_map/ppermute | solution.py:45
  29.8 23.4 %collective-permute-start.2 = (f32[4,16,1]{2,1,0:T(8,128)S(1)}, f32[4,16,1]{2,1,0:T(8,128)S(1)}, u32[]{:S(2)}, u32[]{:S(2)}) collective-permute-start(f32[4,16,1]{2,1,0:T(8,128)S(1)} %get-tuple-element.41), channel_id=1, source_target_pairs={{64,0},{128,64},{192,128},{65,1},{129,65},{193,129},{66,2},{130,66... | collective-permute-start | bytes 776 | tf_op jit(solution)/shard_map/ppermute | solution.py:46
  38.4 11.9 %copy-start.1 = (f32[64,41,1,1,256]{4,1,0,3,2:T(8,128)}, f32[64,41,1,1,256]{4,1,0,3,2:T(8,128)S(1)}, u32[]{:S(2)}) copy-start(f32[64,41,1,1,256]{4,1,0,3,2:T(8,128)S(1)} %fusion) | copy-start | bytes 8060932
  38.4 10.3 %copy-start.3 = (s32[4,16,256]{2,1,0:T(8,128)S(1)}, s32[4,16,256]{2,1,0:T(8,128)}, u32[]{:S(2)}) copy-start(s32[4,16,256]{2,1,0:T(8,128)} %param.14) | copy-start | bytes 196612
  39.4 45.6 %all-to-all-start = ((f32[64,16,1,1,256]{4,1,3,2,0:T(8,128)}), f32[64,16,1,1,256]{4,1,3,2,0:T(8,128)}, u32[]{:S(2)}, u32[]{:S(2)}) async-start(f32[64,16,1,1,256]{4,1,3,2,0:T(8,128)} %slice_bitcast_fusion), calls=%async_computation | async-start | bytes 2097152 | tf_op jit(solution)/shard_map/all_to_all | solution.py:33
  50.4 5.1 %collective-permute-start.1 = (f32[4,16,1]{2,1,0:T(8,128)S(1)}, f32[4,16,1]{2,1,0:T(8,128)S(1)}, u32[]{:S(2)}, u32[]{:S(2)}) collective-permute-start(f32[4,16,1]{2,1,0:T(8,128)S(1)} %get-tuple-element.42), channel_id=1, source_target_pairs={{0,64},{64,128},{128,192},{1,65},{65,129},{129,193},{2,66},{66,130... | collective-permute-start | bytes 776 | tf_op jit(solution)/shard_map/ppermute | solution.py:45
  56.4 25.1 %slice-start = ((f32[64,41,1,1,256]{4,1,0,3,2:T(8,128)}), f32[64,25,1,1,256]{4,1,0,3,2:T(8,128)S(1)}, s32[]{:S(2)}) async-start(f32[64,41,1,1,256]{4,1,0,3,2:T(8,128)} %copy-done.1), calls=%async_computation.2 | async-start | bytes 4194304 | tf_op jit(solution)/shard_map/split | solution.py:31
  62.3 22.5 %copy-start.32 = (f32[4]{0:T(128)S(1)}, f32[4]{0:T(128)}, u32[]{:S(2)}) copy-start(f32[4]{0:T(128)} %get-tuple-element.70) | copy-start | bytes 52
  62.3 22.5 %copy-start.33 = (f32[4]{0:T(128)S(1)}, f32[4]{0:T(128)}, u32[]{:S(2)}) copy-start(f32[4]{0:T(128)} %get-tuple-element.71) | copy-start | bytes 52
  62.3 22.5 %copy-start.34 = (f32[16]{0:T(128)S(1)}, f32[16]{0:T(128)}, u32[]{:S(2)}) copy-start(f32[16]{0:T(128)} %get-tuple-element.68) | copy-start | bytes 196
  62.3 22.5 %copy-start.35 = (f32[16]{0:T(128)S(1)}, f32[16]{0:T(128)}, u32[]{:S(2)}) copy-start(f32[16]{0:T(128)} %get-tuple-element.69) | copy-start | bytes 196
  62.3 17.8 %collective-permute-start.9 = (f32[4,1,256]{2,1,0:T(1,128)S(1)}, f32[4,1,256]{2,1,0:T(1,128)S(1)}, u32[]{:S(2)}, u32[]{:S(2)}) collective-permute-start(f32[4,1,256]{2,1,0:T(1,128)S(1)} %get-tuple-element.33), channel_id=1, source_target_pairs={{8,0},{16,8},{24,16},{32,24},{40,32},{48,40},{56,48},{9,1},{17,9},... | collective-permute-start | bytes 12296 | tf_op jit(solution)/shard_map/ppermute | solution.py:46
  65.3 19.2 %collective-permute-start.6 = (f32[4,1,256]{2,1,0:T(1,128)S(1)}, f32[4,1,256]{2,1,0:T(1,128)S(1)}, u32[]{:S(2)}, u32[]{:S(2)}) collective-permute-start(f32[4,1,256]{2,1,0:T(1,128)S(1)} %get-tuple-element.34), channel_id=1, source_target_pairs={{0,8},{8,16},{16,24},{24,32},{32,40},{40,48},{48,56},{1,9},{9,17},... | collective-permute-start | bytes 12296 | tf_op jit(solution)/shard_map/ppermute | solution.py:45
  70.6 14.2 %collective-permute-start.10 = (f32[1,16,256]{2,1,0:T(8,128)S(1)}, f32[1,16,256]{2,1,0:T(8,128)S(1)}, u32[]{:S(2)}, u32[]{:S(2)}) collective-permute-start(f32[1,16,256]{2,1,0:T(8,128)S(1)} %get-tuple-element.31), channel_id=1, source_target_pairs={{1,0},{2,1},{3,2},{4,3},{5,4},{6,5},{7,6},{9,8},{10,9},{11,10},{12... | collective-permute-start | bytes 49160 | tf_op jit(solution)/shard_map/ppermute | solution.py:46
  73.1 11.8 %collective-permute-start.11 = (f32[1,16,256]{2,1,0:T(8,128)S(1)}, f32[1,16,256]{2,1,0:T(8,128)S(1)}, u32[]{:S(2)}, u32[]{:S(2)}) collective-permute-start(f32[1,16,256]{2,1,0:T(8,128)S(1)} %get-tuple-element.32), channel_id=1, source_target_pairs={{0,1},{1,2},{2,3},{3,4},{4,5},{5,6},{6,7},{8,9},{9,10},{10,11},{11... | collective-permute-start | bytes 49160 | tf_op jit(solution)/shard_map/ppermute | solution.py:45
  78.1 6.5 %collective-permute-start.8 = (f32[4,16,1]{2,1,0:T(8,128)S(1)}, f32[4,16,1]{2,1,0:T(8,128)S(1)}, u32[]{:S(2)}, u32[]{:S(2)}) collective-permute-start(f32[4,16,1]{2,1,0:T(8,128)S(1)} %get-tuple-element.35), channel_id=1, source_target_pairs={{64,0},{128,64},{192,128},{65,1},{129,65},{193,129},{66,2},{130,66... | collective-permute-start | bytes 776 | tf_op jit(solution)/shard_map/ppermute | solution.py:46
  80.1 4.7 %collective-permute-start.7 = (f32[4,16,1]{2,1,0:T(8,128)S(1)}, f32[4,16,1]{2,1,0:T(8,128)S(1)}, u32[]{:S(2)}, u32[]{:S(2)}) collective-permute-start(f32[4,16,1]{2,1,0:T(8,128)S(1)} %get-tuple-element.36), channel_id=1, source_target_pairs={{0,64},{64,128},{128,192},{1,65},{65,129},{129,193},{2,66},{66,130... | collective-permute-start | bytes 776 | tf_op jit(solution)/shard_map/ppermute | solution.py:45
  84.3 9.9 %copy-start.5 = (f32[40]{0:T(128)S(1)}, f32[40]{0:T(128)}, u32[]{:S(2)}) copy-start(f32[40]{0:T(128)} %copy-done.4) | copy-start | bytes 484
  84.3 9.9 %copy-start.7 = (f32[40]{0:T(128)S(1)}, f32[40]{0:T(128)}, u32[]{:S(2)}) copy-start(f32[40]{0:T(128)} %copy-done.6) | copy-start | bytes 484
  84.3 9.9 %copy-start.9 = (f32[40]{0:T(128)S(1)}, f32[40]{0:T(128)}, u32[]{:S(2)}) copy-start(f32[40]{0:T(128)} %copy-done.8) | copy-start | bytes 484
  84.3 9.9 %copy-start.11 = (f32[40]{0:T(128)S(1)}, f32[40]{0:T(128)}, u32[]{:S(2)}) copy-start(f32[40]{0:T(128)} %copy-done.10) | copy-start | bytes 484
  84.3 9.9 %copy-start.13 = (f32[40]{0:T(128)S(1)}, f32[40]{0:T(128)}, u32[]{:S(2)}) copy-start(f32[40]{0:T(128)} %copy-done.12) | copy-start | bytes 484
  84.3 9.9 %copy-start.15 = (f32[40]{0:T(128)S(1)}, f32[40]{0:T(128)}, u32[]{:S(2)}) copy-start(f32[40]{0:T(128)} %copy-done.14) | copy-start | bytes 484
  84.3 9.9 %copy-start.17 = (f32[40]{0:T(128)S(1)}, f32[40]{0:T(128)}, u32[]{:S(2)}) copy-start(f32[40]{0:T(128)} %copy-done.16) | copy-start | bytes 484
  84.3 9.9 %copy-start.19 = (f32[40]{0:T(128)S(1)}, f32[40]{0:T(128)}, u32[]{:S(2)}) copy-start(f32[40]{0:T(128)} %copy-done.18) | copy-start | bytes 484
  84.4 9.9 %copy-start.21 = (f32[40]{0:T(128)S(1)}, f32[40]{0:T(128)}, u32[]{:S(2)}) copy-start(f32[40]{0:T(128)} %copy-done.20) | copy-start | bytes 484
  84.4 9.9 %copy-start.23 = (f32[40]{0:T(128)S(1)}, f32[40]{0:T(128)}, u32[]{:S(2)}) copy-start(f32[40]{0:T(128)} %copy-done.22) | copy-start | bytes 484
  84.4 9.9 %copy-start.25 = (f32[40]{0:T(128)S(1)}, f32[40]{0:T(128)}, u32[]{:S(2)}) copy-start(f32[40]{0:T(128)} %copy-done.24) | copy-start | bytes 484
  84.4 9.9 %copy-start.27 = (f32[40]{0:T(128)S(1)}, f32[40]{0:T(128)}, u32[]{:S(2)}) copy-start(f32[40]{0:T(128)} %copy-done.26) | copy-start | bytes 484
  84.4 9.9 %copy-start.29 = (f32[40]{0:T(128)S(1)}, f32[40]{0:T(128)}, u32[]{:S(2)}) copy-start(f32[40]{0:T(128)} %copy-done.28) | copy-start | bytes 484
  84.4 9.9 %copy-start.31 = (f32[40]{0:T(128)S(1)}, f32[40]{0:T(128)}, u32[]{:S(2)}) copy-start(f32[40]{0:T(128)} %copy-done.30) | copy-start | bytes 484
  85.1 83.8 %all-to-all-start.1 = ((f32[64,25,1,1,256]{4,3,2,1,0:T(1,128)}), f32[64,25,1,1,256]{4,3,2,1,0:T(1,128)}, u32[]{:S(2)}, u32[]{:S(2)}) async-start(f32[64,25,1,1,256]{4,3,2,1,0:T(1,128)} %copy.22), calls=%async_computation.1 | async-start | bytes 3276800 | tf_op jit(solution)/shard_map/all_to_all | solution.py:33
  98.5 34.7 %collective-permute-start.15 = (f32[4,1,256]{2,1,0:T(1,128)S(1)}, f32[4,1,256]{2,1,0:T(1,128)S(1)}, u32[]{:S(2)}, u32[]{:S(2)}) collective-permute-start(f32[4,1,256]{2,1,0:T(1,128)S(1)} %get-tuple-element.27), channel_id=1, source_target_pairs={{8,0},{16,8},{24,16},{32,24},{40,32},{48,40},{56,48},{9,1},{17,9},... | collective-permute-start | bytes 12296 | tf_op jit(solution)/shard_map/ppermute | solution.py:46
  100.8 33.8 %collective-permute-start.12 = (f32[4,1,256]{2,1,0:T(1,128)S(1)}, f32[4,1,256]{2,1,0:T(1,128)S(1)}, u32[]{:S(2)}, u32[]{:S(2)}) collective-permute-start(f32[4,1,256]{2,1,0:T(1,128)S(1)} %get-tuple-element.28), channel_id=1, source_target_pairs={{0,8},{8,16},{16,24},{24,32},{32,40},{40,48},{48,56},{1,9},{9,17},... | collective-permute-start | bytes 12296 | tf_op jit(solution)/shard_map/ppermute | solution.py:45
  106.2 31.7 %collective-permute-start.16 = (f32[1,16,256]{2,1,0:T(8,128)S(1)}, f32[1,16,256]{2,1,0:T(8,128)S(1)}, u32[]{:S(2)}, u32[]{:S(2)}) collective-permute-start(f32[1,16,256]{2,1,0:T(8,128)S(1)} %get-tuple-element.25), channel_id=1, source_target_pairs={{1,0},{2,1},{3,2},{4,3},{5,4},{6,5},{7,6},{9,8},{10,9},{11,10},{12... | collective-permute-start | bytes 49160 | tf_op jit(solution)/shard_map/ppermute | solution.py:46
  108.7 29.2 %collective-permute-start.17 = (f32[1,16,256]{2,1,0:T(8,128)S(1)}, f32[1,16,256]{2,1,0:T(8,128)S(1)}, u32[]{:S(2)}, u32[]{:S(2)}) collective-permute-start(f32[1,16,256]{2,1,0:T(8,128)S(1)} %get-tuple-element.26), channel_id=1, source_target_pairs={{0,1},{1,2},{2,3},{3,4},{4,5},{5,6},{6,7},{8,9},{9,10},{10,11},{11... | collective-permute-start | bytes 49160 | tf_op jit(solution)/shard_map/ppermute | solution.py:45
  113.7 21.0 %collective-permute-start.14 = (f32[4,16,1]{2,1,0:T(8,128)S(1)}, f32[4,16,1]{2,1,0:T(8,128)S(1)}, u32[]{:S(2)}, u32[]{:S(2)}) collective-permute-start(f32[4,16,1]{2,1,0:T(8,128)S(1)} %get-tuple-element.29), channel_id=1, source_target_pairs={{64,0},{128,64},{192,128},{65,1},{129,65},{193,129},{66,2},{130,66... | collective-permute-start | bytes 776 | tf_op jit(solution)/shard_map/ppermute | solution.py:46
  133.3 4.6 %collective-permute-start.13 = (f32[4,16,1]{2,1,0:T(8,128)S(1)}, f32[4,16,1]{2,1,0:T(8,128)S(1)}, u32[]{:S(2)}, u32[]{:S(2)}) collective-permute-start(f32[4,16,1]{2,1,0:T(8,128)S(1)} %get-tuple-element.30), channel_id=1, source_target_pairs={{0,64},{64,128},{128,192},{1,65},{65,129},{129,193},{2,66},{66,130... | collective-permute-start | bytes 776 | tf_op jit(solution)/shard_map/ppermute | solution.py:45
  142.3 18.1 %collective-permute-start.21 = (f32[4,1,256]{2,1,0:T(1,128)S(1)}, f32[4,1,256]{2,1,0:T(1,128)S(1)}, u32[]{:S(2)}, u32[]{:S(2)}) collective-permute-start(f32[4,1,256]{2,1,0:T(1,128)S(1)} %get-tuple-element.21), channel_id=1, source_target_pairs={{8,0},{16,8},{24,16},{32,24},{40,32},{48,40},{56,48},{9,1},{17,9},... | collective-permute-start | bytes 12296 | tf_op jit(solution)/shard_map/ppermute | solution.py:46
  144.2 17.5 %collective-permute-start.18 = (f32[4,1,256]{2,1,0:T(1,128)S(1)}, f32[4,1,256]{2,1,0:T(1,128)S(1)}, u32[]{:S(2)}, u32[]{:S(2)}) collective-permute-start(f32[4,1,256]{2,1,0:T(1,128)S(1)} %get-tuple-element.22), channel_id=1, source_target_pairs={{0,8},{8,16},{16,24},{24,32},{32,40},{40,48},{48,56},{1,9},{9,17},... | collective-permute-start | bytes 12296 | tf_op jit(solution)/shard_map/ppermute | solution.py:45
  150.0 15.0 %collective-permute-start.22 = (f32[1,16,256]{2,1,0:T(8,128)S(1)}, f32[1,16,256]{2,1,0:T(8,128)S(1)}, u32[]{:S(2)}, u32[]{:S(2)}) collective-permute-start(f32[1,16,256]{2,1,0:T(8,128)S(1)} %get-tuple-element.19), channel_id=1, source_target_pairs={{1,0},{2,1},{3,2},{4,3},{5,4},{6,5},{7,6},{9,8},{10,9},{11,10},{12... | collective-permute-start | bytes 49160 | tf_op jit(solution)/shard_map/ppermute | solution.py:46
  152.5 12.5 %collective-permute-start.23 = (f32[1,16,256]{2,1,0:T(8,128)S(1)}, f32[1,16,256]{2,1,0:T(8,128)S(1)}, u32[]{:S(2)}, u32[]{:S(2)}) collective-permute-start(f32[1,16,256]{2,1,0:T(8,128)S(1)} %get-tuple-element.20), channel_id=1, source_target_pairs={{0,1},{1,2},{2,3},{3,4},{4,5},{5,6},{6,7},{8,9},{9,10},{10,11},{11... | collective-permute-start | bytes 49160 | tf_op jit(solution)/shard_map/ppermute | solution.py:45
  157.5 4.4 %collective-permute-start.20 = (f32[4,16,1]{2,1,0:T(8,128)S(1)}, f32[4,16,1]{2,1,0:T(8,128)S(1)}, u32[]{:S(2)}, u32[]{:S(2)}) collective-permute-start(f32[4,16,1]{2,1,0:T(8,128)S(1)} %get-tuple-element.23), channel_id=1, source_target_pairs={{64,0},{128,64},{192,128},{65,1},{129,65},{193,129},{66,2},{130,66... | collective-permute-start | bytes 776 | tf_op jit(solution)/shard_map/ppermute | solution.py:46
  160.4 4.7 %collective-permute-start.19 = (f32[4,16,1]{2,1,0:T(8,128)S(1)}, f32[4,16,1]{2,1,0:T(8,128)S(1)}, u32[]{:S(2)}, u32[]{:S(2)}) collective-permute-start(f32[4,16,1]{2,1,0:T(8,128)S(1)} %get-tuple-element.24), channel_id=1, source_target_pairs={{0,64},{64,128},{128,192},{1,65},{65,129},{129,193},{2,66},{66,130... | collective-permute-start | bytes 776 | tf_op jit(solution)/shard_map/ppermute | solution.py:45
where the time goes:
time: 177 us; the launch traced here: 175 us
  starting transfers between devices  94.8 us (54%)
  other arithmetic  29.6 us (17%)
  waiting for transfers between devices  25.5 us (14%)
  local copies, waits for them, and re-layouts  23.1 us (13%)
    ppermute x12, starting transfers between devices, extended(): lax.ppermute(last, axis, up)  47.2 us
    ppermute x12, starting transfers between devices, extended(): lax.ppermute(first, axis, [(b, a) for a, b in up])  29.8 us
    reduce_sum x4, other arithmetic, per_device(): jnp.sum(cond_cells * gate_states * (voltage[None] - rev_cells), axis=0)  20.9 us
    all_to_all x2, starting transfers between devices, cut_exchange(): lax.all_to_all(share, axis, split_axis=0, concat_axis=0, tiled=True)  17.8 us
    ppermute x12, waiting for transfers between devices, extended(): lax.ppermute(first, axis, [(b, a) for a, b in up])  16.7 us
    ppermute x12, waiting for transfers between devices, extended(): lax.ppermute(last, axis, up)  8.86 us
    unnamed x77, local copies, waits for them, and re-layouts  6.05 us
    split x4, local copies, waits for them, and re-layouts, cut_exchange(): jnp.split(parts, cut_rows(parts.shape[widest], pieces), axis=widest)  3.89 us
  transfers between devices with their start and end apart: 26, of which 5 were waited for; matrix products, arithmetic and copies ran while one was open for 20% of the time, Pallas kernels for 0%

commit v1 on v0

v1 whole, which is shorter than its diff:
```python
import functools

import jax
import jax.numpy as jnp
from jax import lax
from jax.experimental import pallas as pl
from jax.experimental.pallas import tpu as pltpu
from jax.sharding import PartitionSpec as P

MESH = pl.DeviceIdType.MESH
STEPS = 4
STATES = 41
GATES = 40
LAYERS = 3
FIBERS = 16
CT, CW, CD = 4, 16, 256
ROWS = CT * CW
WRITERS = 64
GROUPS = ((1, 17), (17, 33), (33, 49), (49, 64))
LOG2E = 1.4426950408889634


def place(i):
    gy, gz = lax.axis_index("gy"), lax.axis_index("gz")
    j = lax.rem(i * 27, 64)
    z = lax.rem((gy // 2) * 2 + gz // 4 + lax.rem(j, 8), 8)
    x = lax.rem(lax.rem(gz, 4) + lax.rem(j // 8, 4), 4)
    core = lax.rem(lax.rem(gy, 2) + j // 32, 2)
    return (z // 2) * 2 + core, lax.rem(z, 2) * 4 + x


def kernel(
    states,
    prior,
    layers_in,
    fibers_in,
    writer_stripe,
    gate_half,
    gate_slope,
    gate_tau,
    gate_conduct,
    gate_reversal,
    fiber_conduct,
    new_states,
    stripes,
    held,
    send,
    layers,
    fibers,
    table,
    sigma,
    excited,
    width_out,
    across_in,
    width_in,
    depth_in,
    load_sem,
    piece_send,
    piece_recv,
    face_send,
    face_recv,
):
    gx, gy, gz = (lax.axis_index(a) for a in ("gx", "gy", "gz"))
    me = gy * 8 + gz

    def neighbour(axis, up):
        size = lax.axis_size(axis)
        return lax.rem(lax.axis_index(axis) + (1 if up else size - 1), size)

    barrier = pltpu.get_barrier_semaphore()

    def greet(i, carry):
        a, b = place(i)
        pl.semaphore_signal(barrier, inc=1, device_id={"gy": a, "gz": b}, device_id_type=MESH)
        return carry

    for up in (False, True):
        pl.semaphore_signal(
            barrier, inc=1, device_id={"gx": neighbour("gx", up)}, device_id_type=MESH
        )
    lax.fori_loop(1, WRITERS, greet, 0)

    loads = [
        pltpu.make_async_copy(states, new_states, load_sem.at[0]),
        pltpu.make_async_copy(layers_in, layers, load_sem.at[1]),
        pltpu.make_async_copy(fibers_in, fibers, load_sem.at[2]),
    ] + [
        pltpu.make_async_copy(
            prior.at[:, :, pl.ds(128 * half, 128)], held.at[:, half], load_sem.at[3 + half]
        )
        for half in range(2)
    ]
    for load in loads:
        load.start()

    def pieces(first, last):
        rows = held.reshape(STATES * 2 * ROWS, 128)

        def one(i, carry):
            a, b = place(i)
            piece = writer_stripe[a * 8 + b]
            for s in range(STATES):
                send[i, s] = rows[pl.ds(piece + s * 2 * ROWS, 2, stride=ROWS), :]
            return carry

        lax.fori_loop(first, last, one, 0)

    def own_piece():
        rows = held.reshape(STATES * 2 * ROWS, 128)
        piece = writer_stripe[me]
        for s in range(STATES):
            stripes[s, me] = rows[pl.ds(piece + s * 2 * ROWS, 2, stride=ROWS), :]

    def piece_copy(i):
        a, b = place(i)
        return pltpu.make_async_remote_copy(
            src_ref=send.at[i],
            dst_ref=stripes.at[:, me],
            send_sem=piece_send.at[i],
            recv_sem=piece_recv.at[me],
            device_id={"gy": a, "gz": b},
            device_id_type=MESH,
        )

    def send_pieces(first, last):
        def one(i, carry):
            piece_copy(i).start()
            return carry

        lax.fori_loop(first, last, one, 0)

    def face_copies(step):
        u = excited.at[step]
        plan = []
        for up in (False, True):
            side = int(up)
            plan.append((u.at[pl.ds(48 if up else 0, 16), :], across_in.at[step, side], "gz", up))
            plan.append((width_out.at[step, side], width_in.at[step, side], "gy", up))
            plan.append((u.at[:, pl.ds(128 if up else 0, 128)], depth_in.at[step, side], "gx", up))
        return [
            pltpu.make_async_remote_copy(
                src_ref=src,
                dst_ref=dst,
                send_sem=face_send.at[step * 6 + n],
                recv_sem=face_recv.at[step * 6 + n],
                device_id={axis: neighbour(axis, up)},
                device_id_type=MESH,
            )
            for n, (src, dst, axis, up) in enumerate(plan)
        ]

    def build_tables():
        def one(g, carry):
            half = [gate_half[n, g] for n in range(LAYERS)]
            slope = [gate_slope[n, g] for n in range(LAYERS)]
            tau = [gate_tau[n, g] for n in range(LAYERS)]
            conduct = [gate_conduct[n, g] for n in range(LAYERS)]
            reversal = [gate_reversal[n, g] for n in range(LAYERS)]
            for part in range(2):
                at = pl.ds(part * 32, 32)
                kind = layers[at, :]
                first, second = kind == 0, kind == 1
                for n, of in enumerate((half, slope, tau, conduct, reversal)):
                    value = jnp.where(first, of[0], jnp.where(second, of[1], of[2]))
                    if n == 1:
                        value = -value
                    if n == 2:
                        value = -1.0 / value
                    table[g, n, at, :] = value
            return carry

        lax.fori_loop(0, GATES, one, 0)
        kind = fibers[...]
        for c in range(3):
            value = jnp.full((ROWS, CD), fiber_conduct[FIBERS - 1, c], jnp.float32)
            for f in range(FIBERS - 2, -1, -1):
                value = jnp.where(kind == f, fiber_conduct[f, c], value)
            sigma[c] = value

    def ionic(step):
        for part in range(2):
            at = pl.ds(part * 32, 32)
            voltage = new_states[0, at, :]

            def one(g, current):
                grown = jnp.exp((voltage - table[g, 0, at, :]) * table[g, 1, at, :])
                steady = 1.0 / (1.0 + grown)
                decay = jnp.exp(table[g, 2, at, :] * (1.0 - 1.0 / (2.0 + grown)))
                gate = steady + (new_states[1 + g, at, :] - steady) * decay
                new_states[1 + g, at, :] = gate
                return current + table[g, 3, at, :] * gate * (voltage - table[g, 4, at, :])

            current = lax.fori_loop(0, GATES, one, jnp.zeros((32, CD), jnp.float32))
            excited[step, at, :] = voltage - current
        for t in range(CT):
            width_out[step, 0, pl.ds(t, 1), :] = excited[step, pl.ds(t * CW, 1), :]
            width_out[step, 1, pl.ds(t, 1), :] = excited[step, pl.ds(t * CW + CW - 1, 1), :]

    row = lax.broadcasted_iota(jnp.int32, (CW, CD), 0)
    lane = lax.broadcasted_iota(jnp.int32, (CW, 128), 1)
    gx_low, gx_high = gx == 0, gx == lax.axis_size("gx") - 1
    gy_low, gy_high = gy == 0, gy == lax.axis_size("gy") - 1
    gz_low, gz_high = gz == 0, gz == lax.axis_size("gz") - 1

    def diffuse(step):
        for t in range(CT):
            at = pl.ds(t * CW, CW)
            here = excited[step, at, :]
            if t == 0:
                below = jnp.where(gz_low, here, across_in[step, 1])
            else:
                below = excited[step, pl.ds((t - 1) * CW, CW), :]
            if t == CT - 1:
                above = jnp.where(gz_high, here, across_in[step, 0])
            else:
                above = excited[step, pl.ds((t + 1) * CW, CW), :]
            across = (above - here) + (below - here)

            low = jnp.broadcast_to(width_in[step, 1, pl.ds(t, 1), :], (CW, CD))
            high = jnp.broadcast_to(width_in[step, 0, pl.ds(t, 1), :], (CW, CD))
            low = jnp.where(gy_low, here, low)
            high = jnp.where(gy_high, here, high)
            below = jnp.where(row == 0, low, pltpu.roll(here, 1, 0))
            above = jnp.where(row == CW - 1, high, pltpu.roll(here, CW - 1, 0))
            widthwise = (above - here) + (below - here)

            left, right = here[:, :128], here[:, 128:]
            before = pltpu.roll(depth_in[step, 1, at, :], 1, 1)
            after = pltpu.roll(depth_in[step, 0, at, :], 127, 1)
            before = jnp.where(gx_low, left, before)
            after = jnp.where(gx_high, right, after)
            left_up, right_up = pltpu.roll(left, 1, 1), pltpu.roll(right, 1, 1)
            left_down, right_down = pltpu.roll(left, 127, 1), pltpu.roll(right, 127, 1)
            below = (jnp.where(lane == 0, before, left_up), jnp.where(lane == 0, left_up, right_up))
            above = (
                jnp.where(lane == 127, right_down, left_down),
                jnp.where(lane == 127, after, right_down),
            )
            part = excited[step, at, :] + sigma[0, at, :] * across + sigma[1, at, :] * widthwise
            for half, mid in enumerate((left, right)):
                lanes = pl.ds(128 * half, 128)
                depthwise = (above[half] - mid) + (below[half] - mid)
                new_states[0, at, lanes] = (
                    part[:, 128 * half : 128 * half + 128] + sigma[2, at, lanes] * depthwise
                )

    loads[1].wait()
    loads[2].wait()
    build_tables()
    loads[0].wait()
    ionic(0)
    loads[3].wait()
    loads[4].wait()
    pieces(*GROUPS[0])
    pl.semaphore_wait(barrier, WRITERS + 1)
    for step in range(STEPS):
        faces = face_copies(step)
        for face in faces:
            face.start()
        send_pieces(*GROUPS[step])
        if step + 1 < STEPS:
            pieces(*GROUPS[step + 1])
        else:
            own_piece()
        for face in faces:
            face.wait_recv()
        diffuse(step)
        if step + 1 < STEPS:
            ionic(step + 1)

    def drain(i, carry):
        copy = piece_copy(i)
        copy.wait_send()
        a, b = place(i)
        pltpu.make_async_remote_copy(
            src_ref=send.at[i],
            dst_ref=stripes.at[:, a * 8 + b],
            send_sem=piece_send.at[i],
            recv_sem=piece_recv.at[a * 8 + b],
            device_id={"gy": a, "gz": b},
            device_id_type=MESH,
        ).wait_recv()
        return carry

    lax.fori_loop(1, WRITERS, drain, 0)
    for step in range(STEPS):
        for face in face_copies(step):
            face.wait_send()


def per_device(
    states,
    prior_states,
    cell_layers,
    fiber_classes,
    writer_stripe,
    gate_half,
    gate_slope,
    gate_tau,
    gate_conduct,
    gate_reversal,
    fiber_conduct,
):
    f32 = jnp.float32
    anywhere = pl.BlockSpec(memory_space=pl.ANY)
    scalars = pl.BlockSpec(memory_space=pltpu.SMEM)
    vmem = pl.BlockSpec(memory_space=pltpu.VMEM)
    new_states, stripes = pl.pallas_call(
        kernel,
        out_shape=(
            jax.ShapeDtypeStruct((STATES, ROWS, CD), f32),
            jax.ShapeDtypeStruct((STATES, WRITERS, 2, 128), f32),
        ),
        in_specs=[anywhere] * 4 + [scalars] * 7,
        out_specs=(vmem, vmem),
        scratch_shapes=[
            pltpu.VMEM((STATES, 2, ROWS, 128), f32),
            pltpu.VMEM((WRITERS, STATES, 2, 128), f32),
            pltpu.VMEM((ROWS, CD), jnp.int32),
            pltpu.VMEM((ROWS, CD), jnp.int32),
            pltpu.VMEM((GATES, 5, ROWS, CD), f32),
            pltpu.VMEM((3, ROWS, CD), f32),
            pltpu.VMEM((STEPS, ROWS, CD), f32),
            pltpu.VMEM((STEPS, 2, CT, CD), f32),
            pltpu.VMEM((STEPS, 2, CW, CD), f32),
            pltpu.VMEM((STEPS, 2, CT, CD), f32),
            pltpu.VMEM((STEPS, 2, ROWS, 128), f32),
            pltpu.SemaphoreType.DMA((5,)),
            pltpu.SemaphoreType.DMA((WRITERS,)),
            pltpu.SemaphoreType.DMA((WRITERS,)),
            pltpu.SemaphoreType.DMA((STEPS * 6,)),
            pltpu.SemaphoreType.DMA((STEPS * 6,)),
        ],
        compiler_params=pltpu.CompilerParams(collective_id=0, has_side_effects=True, vmem_limit_bytes=40 * 1024 * 1024),
    )(
        states.reshape(STATES, ROWS, CD),
        prior_states.reshape(STATES, ROWS, CD),
        cell_layers.reshape(ROWS, CD),
        fiber_classes.reshape(ROWS, CD),
        writer_stripe,
        gate_half,
        gate_slope,
        gate_tau,
        gate_conduct,
        gate_reversal,
        fiber_conduct,
    )
    return new_states.reshape(states.shape), stripes.reshape(STATES, WRITERS, 1, CD)


def solution(mesh):
    cells = P(None, "gz", "gy", "gx")
    in_specs = (cells, cells, P("gz", "gy", "gx"), P("gz", "gy", "gx")) + (P(),) * 7
    out_specs = (cells, P(None, ("gy", "gz"), None, "gx"))
    return jax.shard_map(
        per_device, mesh=mesh, in_specs=in_specs, out_specs=out_specs, check_vma=False
    )
```

time: 177 us -> 95.6 us (0.54)
  the two profiles are of different devices: /device:TPU:95 before, /device:TPU:1 now
where the time goes in v1:
time: 95.6 us; the launch traced here: 95 us
  Pallas kernels  81.3 us (85%)
  local copies, waits for them, and re-layouts  13 us (14%)
    pallas_call x1, Pallas kernels, per_device(): pl.pallas_call(kernel, out_shape=(jax.ShapeDtypeStruct((STATES, ROWS, CD)...  81.3 us
    unnamed x23, local copies, waits for them, and re-layouts  13 us

profile of v1, /device:TPU:1, one launch (start us, length us, event | category | flops | bytes accessed | tf_op | source)
XLA Modules:
  0.0 95.0 jit_solution(14439950654858032285)
XLA Ops:
  0.6 0.8 copy.13.fiber_conduct
  1.4 0.0 copy-start
  1.4 1.8 %copy-done = f32[41,4,16,256]{3,2,1,0:T(8,128)S(1)} copy-done((f32[41,4,16,256]{3,2,1,0:T(8,128)S(1)}, f32[41,4,16,256]{3,2,1,0:T(8,128)}, u32[]{:S(2)}) %copy-start) | copy-done | bytes 2687000
  3.1 0.0 copy-start.1
  3.1 1.8 %copy-done.1 = f32[41,4,16,256]{3,2,1,0:T(8,128)S(1)} copy-done((f32[41,4,16,256]{3,2,1,0:T(8,128)S(1)}, f32[41,4,16,256]{3,2,1,0:T(8,128)}, u32[]{:S(2)}) %copy-start.1) | copy-done | bytes 2687000
  4.9 0.0 copy-start.2
  4.9 0.8 copy-done.2
  5.7 0.0 copy-start.3
  5.7 0.8 copy-done.3
  6.6 0.0 copy-start.4
  6.6 0.7 copy-done.4
  7.3 0.0 copy-start.5
  7.3 0.7 copy-done.5
  8.0 0.0 copy-start.6
  8.0 0.7 copy-done.6
  8.6 0.0 copy-start.7
  8.6 0.7 copy-done.7
  9.3 0.0 copy-start.8
  9.3 0.7 copy-done.8
  10.0 0.0 copy-start.9
  10.0 0.7 copy-done.9
  10.7 81.3 %shard_map.122 = (f32[41,64,256]{2,1,0:T(8,128)S(1)}, f32[41,64,2,128]{3,2,1,0:T(2,128)S(1)}) custom-call(f32[41,64,256]{2,1,0:T(8,128)S(1)} %bitcast.6, f32[41,64,256]{2,1,0:T(8,128)S(1)} %bitcast.7, s32[64,256]{1,0:T(8,128)S(1)} %bitcast.10, s32[64,256]{1,0:T(8,128)S(1)} %bitcast.11, s32[64]{0:T(128)S(1)} %copy-done.9, f32[3,40]{1,0:T(4,128)S(1)} %copy-done.4, ...), custom_call_target="tpu_custom_call" | custom-call | tf_op jit(solution)/shard_map/pallas_call | solution.py:308
  92.0 1.5 %copy.17 = f32[41,4,16,256]{3,2,1,0:T(8,128)} copy(f32[41,4,16,256]{3,2,1,0:T(8,128)S(1)} %bitcast.9) | data formatting | bytes 5373952
  93.5 1.5 %copy.18 = f32[41,64,1,256]{3,2,1,0:T(1,128)} copy(f32[41,64,1,256]{3,2,1,0:T(1,128)S(1)} %bitcast.8) | data formatting | bytes 5373952
Async XLA Ops:
  1.4 1.8 %copy-start = (f32[41,4,16,256]{3,2,1,0:T(8,128)S(1)}, f32[41,4,16,256]{3,2,1,0:T(8,128)}, u32[]{:S(2)}) copy-start(f32[41,4,16,256]{3,2,1,0:T(8,128)} %param.11) | copy-start | bytes 8060932
  3.1 1.8 %copy-start.1 = (f32[41,4,16,256]{3,2,1,0:T(8,128)S(1)}, f32[41,4,16,256]{3,2,1,0:T(8,128)}, u32[]{:S(2)}) copy-start(f32[41,4,16,256]{3,2,1,0:T(8,128)} %param.12) | copy-start | bytes 8060932
  4.9 0.8 copy-start.2
  5.7 0.8 copy-start.3
  6.6 0.7 copy-start.4
  7.3 0.7 copy-start.5
  8.0 0.7 copy-start.6
  8.6 0.7 copy-start.7
  9.3 0.7 copy-start.8
  10.0 0.7 copy-start.9

commit v2 on v1

--- a/solution.py
+++ b/solution.py
@@ -16,7 +16,7 @@
 CT, CW, CD = 4, 16, 256
 ROWS = CT * CW
 WRITERS = 64
-GROUPS = ((1, 17), (17, 33), (33, 49), (49, 64))
+CUTS = (1, 12, 23, 34, 45, 64)
 LOG2E = 1.4426950408889634
 
 
@@ -34,6 +34,15 @@
     prior,
     layers_in,
     fibers_in,
+    writer_stripe_in,
+    gate_half_in,
+    gate_slope_in,
+    gate_tau_in,
+    gate_conduct_in,
+    gate_reversal_in,
+    fiber_conduct_in,
+    new_states,
+    stripes,
     writer_stripe,
     gate_half,
     gate_slope,
@@ -41,8 +50,6 @@
     gate_conduct,
     gate_reversal,
     fiber_conduct,
-    new_states,
-    stripes,
     held,
     send,
     layers,
@@ -80,18 +87,30 @@
         )
     lax.fori_loop(1, WRITERS, greet, 0)
 
-    loads = [
-        pltpu.make_async_copy(states, new_states, load_sem.at[0]),
-        pltpu.make_async_copy(layers_in, layers, load_sem.at[1]),
-        pltpu.make_async_copy(fibers_in, fibers, load_sem.at[2]),
-    ] + [
-        pltpu.make_async_copy(
-            prior.at[:, :, pl.ds(128 * half, 128)], held.at[:, half], load_sem.at[3 + half]
+    def load(source, target, n):
+        copy = pltpu.make_async_copy(source, target, load_sem.at[n])
+        copy.start()
+        return copy
+
+    piece_loads = [load(writer_stripe_in, writer_stripe, 0)] + [
+        load(prior.at[:, :, pl.ds(128 * half, 128)], held.at[:, half], 1 + half) for half in range(2)
+    ]
+    table_loads = [
+        load(source, target, 3 + n)
+        for n, (source, target) in enumerate(
+            (
+                (layers_in, layers),
+                (gate_half_in, gate_half),
+                (gate_slope_in, gate_slope),
+                (gate_tau_in, gate_tau),
+                (gate_conduct_in, gate_conduct),
+                (gate_reversal_in, gate_reversal),
+                (fibers_in, fibers),
+                (fiber_conduct_in, fiber_conduct),
+            )
         )
-        for half in range(2)
     ]
-    for load in loads:
-        load.start()
+    state_load = load(states, new_states, 11)
 
     def pieces(first, last):
         rows = held.reshape(STATES * 2 * ROWS, 128)
@@ -172,9 +191,9 @@
         lax.fori_loop(0, GATES, one, 0)
         kind = fibers[...]
         for c in range(3):
-            value = jnp.full((ROWS, CD), fiber_conduct[FIBERS - 1, c], jnp.float32)
+            value = jnp.full((ROWS, CD), fiber_conduct[c, FIBERS - 1], jnp.float32)
             for f in range(FIBERS - 2, -1, -1):
-                value = jnp.where(kind == f, fiber_conduct[f, c], value)
+                value = jnp.where(kind == f, fiber_conduct[c, f], value)
             sigma[c] = value
 
     def ionic(step):
@@ -244,22 +263,24 @@
                     part[:, 128 * half : 128 * half + 128] + sigma[2, at, lanes] * depthwise
                 )
 
-    loads[1].wait()
-    loads[2].wait()
+    for copy in piece_loads:
+        copy.wait()
+    pieces(CUTS[0], CUTS[1])
+    pl.semaphore_wait(barrier, WRITERS + 1)
+    send_pieces(CUTS[0], CUTS[1])
+    pieces(CUTS[1], CUTS[2])
+    for copy in table_loads:
+        copy.wait()
     build_tables()
-    loads[0].wait()
+    state_load.wait()
     ionic(0)
-    loads[3].wait()
-    loads[4].wait()
-    pieces(*GROUPS[0])
-    pl.semaphore_wait(barrier, WRITERS + 1)
     for step in range(STEPS):
         faces = face_copies(step)
         for face in faces:
             face.start()
-        send_pieces(*GROUPS[step])
+        send_pieces(CUTS[step + 1], CUTS[step + 2])
         if step + 1 < STEPS:
-            pieces(*GROUPS[step + 1])
+            pieces(CUTS[step + 2], CUTS[step + 3])
         else:
             own_piece()
         for face in faces:
@@ -302,18 +323,24 @@
     fiber_conduct,
 ):
     f32 = jnp.float32
-    anywhere = pl.BlockSpec(memory_space=pl.ANY)
-    scalars = pl.BlockSpec(memory_space=pltpu.SMEM)
+    hbm = pl.BlockSpec(memory_space=pltpu.HBM)
     vmem = pl.BlockSpec(memory_space=pltpu.VMEM)
     new_states, stripes = pl.pallas_call(
         kernel,
         out_shape=(
-            jax.ShapeDtypeStruct((STATES, ROWS, CD), f32),
-            jax.ShapeDtypeStruct((STATES, WRITERS, 2, 128), f32),
+            pltpu.VMEM((STATES, ROWS, CD), f32),
+            pltpu.VMEM((STATES, WRITERS, 2, 128), f32),
         ),
-        in_specs=[anywhere] * 4 + [scalars] * 7,
+        in_specs=[hbm] * 11,
         out_specs=(vmem, vmem),
         scratch_shapes=[
+            pltpu.SMEM((WRITERS,), jnp.int32),
+            pltpu.SMEM((LAYERS, GATES), f32),
+            pltpu.SMEM((LAYERS, GATES), f32),
+            pltpu.SMEM((LAYERS, GATES), f32),
+            pltpu.SMEM((LAYERS, GATES), f32),
+            pltpu.SMEM((LAYERS, GATES), f32),
+            pltpu.SMEM((3, FIBERS), f32),
             pltpu.VMEM((STATES, 2, ROWS, 128), f32),
             pltpu.VMEM((WRITERS, STATES, 2, 128), f32),
             pltpu.VMEM((ROWS, CD), jnp.int32),
@@ -325,25 +352,32 @@
             pltpu.VMEM((STEPS, 2, CW, CD), f32),
             pltpu.VMEM((STEPS, 2, CT, CD), f32),
             pltpu.VMEM((STEPS, 2, ROWS, 128), f32),
-            pltpu.SemaphoreType.DMA((5,)),
+            pltpu.SemaphoreType.DMA((12,)),
             pltpu.SemaphoreType.DMA((WRITERS,)),
             pltpu.SemaphoreType.DMA((WRITERS,)),
             pltpu.SemaphoreType.DMA((STEPS * 6,)),
             pltpu.SemaphoreType.DMA((STEPS * 6,)),
         ],
-        compiler_params=pltpu.CompilerParams(collective_id=0, has_side_effects=True, vmem_limit_bytes=40 * 1024 * 1024),
+        compiler_params=pltpu.CompilerParams(
+            collective_id=0, has_side_effects=True, vmem_limit_bytes=40 * 1024 * 1024
+        ),
     )(
-        states.reshape(STATES, ROWS, CD),
-        prior_states.reshape(STATES, ROWS, CD),
-        cell_layers.reshape(ROWS, CD),
-        fiber_classes.reshape(ROWS, CD),
-        writer_stripe,
-        gate_half,
-        gate_slope,
-        gate_tau,
-        gate_conduct,
-        gate_reversal,
-        fiber_conduct,
+        *(
+            pltpu.with_memory_space_constraint(value, pltpu.HBM)
+            for value in (
+                states.reshape(STATES, ROWS, CD),
+                prior_states.reshape(STATES, ROWS, CD),
+                cell_layers.reshape(ROWS, CD),
+                fiber_classes.reshape(ROWS, CD),
+                writer_stripe,
+                gate_half,
+                gate_slope,
+                gate_tau,
+                gate_conduct,
+                gate_reversal,
+                fiber_conduct.T,
+            )
+        )
     )
     return new_states.reshape(states.shape), stripes.reshape(STATES, WRITERS, 1, CD)
 

time: 95.6 us -> 82 us (0.86)
  local copies, waits for them, and re-layouts: 13 us -> 3.03 us
  Pallas kernels: 81.3 us -> 78.3 us
    unnamed x23 -> x2, local copies, waits for them, and re-layouts: 13 us -> 3.03 us
    pallas_call x1, Pallas kernels: 81.3 us -> 78.3 us  [per_device(): pl.pallas_call(kernel, out_shape=(pltpu.VMEM((STATES, ROWS, CD), f32), pl...]
where the time goes in v2:
time: 82 us; the launch traced here: 81.9 us
  Pallas kernels  78.3 us (95%)
  local copies, waits for them, and re-layouts  3.03 us (4%)
    pallas_call x1, Pallas kernels, per_device(): pl.pallas_call(kernel, out_shape=(pltpu.VMEM((STATES, ROWS, CD), f32), pl...  78.3 us
    unnamed x2, local copies, waits for them, and re-layouts  3.03 us

profile of v2, /device:TPU:1, one launch (start us, length us, event | category | flops | bytes accessed | tf_op | source)
XLA Modules:
  0.0 81.9 jit_solution(16816047597060982660)
XLA Ops:
  0.6 78.3 %shard_map.122 = (f32[41,64,256]{2,1,0:T(8,128)S(1)}, f32[41,64,2,128]{3,2,1,0:T(2,128)S(1)}) custom-call(f32[41,64,256]{2,1,0:T(8,128)} %bitcast.9, f32[41,64,256]{2,1,0:T(8,128)} %bitcast.10, s32[64,256]{1,0:T(8,128)} %bitcast.11, s32[64,256]{1,0:T(8,128)} %bitcast.12, s32[64]{0:T(128)} %writer_stripe_in.1, f32[3,40]{1,0:T(4,128)} %gate_half_in.1, ...), custom_call_target="tpu_custom_call" | custom-call | tf_op jit(solution)/shard_map/pallas_call | solution.py:328
  78.9 1.5 %copy.16 = f32[41,4,16,256]{3,2,1,0:T(8,128)} copy(f32[41,4,16,256]{3,2,1,0:T(8,128)S(1)} %bitcast.8) | data formatting | bytes 5373952
  80.4 1.5 %copy.17 = f32[41,64,1,256]{3,2,1,0:T(1,128)} copy(f32[41,64,1,256]{3,2,1,0:T(1,128)S(1)} %bitcast.7) | data formatting | bytes 5373952

commit v3 on v2

--- a/solution.py
+++ b/solution.py
@@ -20,13 +20,12 @@
 LOG2E = 1.4426950408889634
 
 
-def place(i):
-    gy, gz = lax.axis_index("gy"), lax.axis_index("gz")
-    j = lax.rem(i * 27, 64)
-    z = lax.rem((gy // 2) * 2 + gz // 4 + lax.rem(j, 8), 8)
-    x = lax.rem(lax.rem(gz, 4) + lax.rem(j // 8, 4), 4)
-    core = lax.rem(lax.rem(gy, 2) + j // 32, 2)
-    return (z // 2) * 2 + core, lax.rem(z, 2) * 4 + x
+PARTNERS = tuple((i * 27 % 64 % 8, i * 27 % 64 // 8 % 4, i * 27 % 64 // 32) for i in range(WRITERS))
+
+
+def hops(partner):
+    z, x, _ = PARTNERS[partner]
+    return min(z, 8 - z) + min(x, 4 - x)
 
 
 def kernel(
@@ -50,6 +49,7 @@
     gate_conduct,
     gate_reversal,
     fiber_conduct,
+    chosen,
     held,
     send,
     layers,
@@ -74,18 +74,23 @@
         size = lax.axis_size(axis)
         return lax.rem(lax.axis_index(axis) + (1 if up else size - 1), size)
 
+    layer = [lax.rem((gy // 2) * 2 + gz // 4 + k, 8) for k in range(8)]
+    pair, odd = [(z // 2) * 2 for z in layer], [lax.rem(z, 2) * 4 for z in layer]
+    column = [lax.rem(lax.rem(gz, 4) + k, 4) for k in range(4)]
+    core = [lax.rem(gy + k, 2) for k in range(2)]
+
+    def place(i):
+        z, x, c = PARTNERS[i]
+        return pair[z] + core[c], odd[z] + column[x]
+
     barrier = pltpu.get_barrier_semaphore()
-
-    def greet(i, carry):
+    for i in sorted(range(1, WRITERS), key=hops, reverse=True):
         a, b = place(i)
         pl.semaphore_signal(barrier, inc=1, device_id={"gy": a, "gz": b}, device_id_type=MESH)
-        return carry
-
     for up in (False, True):
         pl.semaphore_signal(
             barrier, inc=1, device_id={"gx": neighbour("gx", up)}, device_id_type=MESH
         )
-    lax.fori_loop(1, WRITERS, greet, 0)
 
     def load(source, target, n):
         copy = pltpu.make_async_copy(source, target, load_sem.at[n])
@@ -116,12 +121,13 @@
         rows = held.reshape(STATES * 2 * ROWS, 128)
 
         def one(i, carry):
+            for s in range(STATES):
+                send[i, s] = rows[pl.ds(chosen[i] + s * 2 * ROWS, 2, stride=ROWS), :]
+            return carry
+
+        for i in range(first, last):
             a, b = place(i)
-            piece = writer_stripe[a * 8 + b]
-            for s in range(STATES):
-                send[i, s] = rows[pl.ds(piece + s * 2 * ROWS, 2, stride=ROWS), :]
-            return carry
-
+            chosen[i] = writer_stripe[a * 8 + b]
         lax.fori_loop(first, last, one, 0)
 
     def own_piece():
@@ -130,23 +136,17 @@
         for s in range(STATES):
             stripes[s, me] = rows[pl.ds(piece + s * 2 * ROWS, 2, stride=ROWS), :]
 
-    def piece_copy(i):
-        a, b = place(i)
-        return pltpu.make_async_remote_copy(
-            src_ref=send.at[i],
-            dst_ref=stripes.at[:, me],
-            send_sem=piece_send.at[i],
-            recv_sem=piece_recv.at[me],
-            device_id={"gy": a, "gz": b},
-            device_id_type=MESH,
-        )
-
     def send_pieces(first, last):
-        def one(i, carry):
-            piece_copy(i).start()
-            return carry
-
-        lax.fori_loop(first, last, one, 0)
+        for i in range(first, last):
+            a, b = place(i)
+            pltpu.make_async_remote_copy(
+                src_ref=send.at[i],
+                dst_ref=stripes.at[:, me],
+                send_sem=piece_send,
+                recv_sem=piece_recv,
+                device_id={"gy": a, "gz": b},
+                device_id_type=MESH,
+            ).start()
 
     def face_copies(step):
         u = excited.at[step]
@@ -289,21 +289,9 @@
         if step + 1 < STEPS:
             ionic(step + 1)
 
-    def drain(i, carry):
-        copy = piece_copy(i)
-        copy.wait_send()
-        a, b = place(i)
-        pltpu.make_async_remote_copy(
-            src_ref=send.at[i],
-            dst_ref=stripes.at[:, a * 8 + b],
-            send_sem=piece_send.at[i],
-            recv_sem=piece_recv.at[a * 8 + b],
-            device_id={"gy": a, "gz": b},
-            device_id_type=MESH,
-        ).wait_recv()
-        return carry
-
-    lax.fori_loop(1, WRITERS, drain, 0)
+    sent = send.at[pl.ds(1, WRITERS - 1)]
+    pltpu.make_async_copy(sent, sent, piece_send).wait()
+    pltpu.make_async_copy(sent, sent, piece_recv).wait()
     for step in range(STEPS):
         for face in face_copies(step):
             face.wait_send()
@@ -341,6 +329,7 @@
             pltpu.SMEM((LAYERS, GATES), f32),
             pltpu.SMEM((LAYERS, GATES), f32),
             pltpu.SMEM((3, FIBERS), f32),
+            pltpu.SMEM((WRITERS,), jnp.int32),
             pltpu.VMEM((STATES, 2, ROWS, 128), f32),
             pltpu.VMEM((WRITERS, STATES, 2, 128), f32),
             pltpu.VMEM((ROWS, CD), jnp.int32),
@@ -353,8 +342,8 @@
             pltpu.VMEM((STEPS, 2, CT, CD), f32),
             pltpu.VMEM((STEPS, 2, ROWS, 128), f32),
             pltpu.SemaphoreType.DMA((12,)),
-            pltpu.SemaphoreType.DMA((WRITERS,)),
-            pltpu.SemaphoreType.DMA((WRITERS,)),
+            pltpu.SemaphoreType.DMA,
+            pltpu.SemaphoreType.DMA,
             pltpu.SemaphoreType.DMA((STEPS * 6,)),
             pltpu.SemaphoreType.DMA((STEPS * 6,)),
         ],

time: 82 us -> 77.6 us (0.946)
  Pallas kernels: 78.3 us -> 73.8 us
    pallas_call x1, Pallas kernels: 78.3 us -> 73.8 us  [per_device(): pl.pallas_call(kernel, out_shape=(pltpu.VMEM((STATES, ROWS, CD), f32), pl...]
where the time goes in v3:
time: 77.6 us; the launch traced here: 77.5 us
  Pallas kernels  73.8 us (95%)
  local copies, waits for them, and re-layouts  3.03 us (4%)
    pallas_call x1, Pallas kernels, per_device(): pl.pallas_call(kernel, out_shape=(pltpu.VMEM((STATES, ROWS, CD), f32), pl...  73.8 us
    unnamed x2, local copies, waits for them, and re-layouts  3.03 us

profile of v3, /device:TPU:1, one launch (start us, length us, event | category | flops | bytes accessed | tf_op | source)
XLA Modules:
  0.0 77.5 jit_solution(206155676307701854)
XLA Ops:
  0.6 73.8 %shard_map.122 = (f32[41,64,256]{2,1,0:T(8,128)S(1)}, f32[41,64,2,128]{3,2,1,0:T(2,128)S(1)}) custom-call(f32[41,64,256]{2,1,0:T(8,128)} %bitcast.9, f32[41,64,256]{2,1,0:T(8,128)} %bitcast.10, s32[64,256]{1,0:T(8,128)} %bitcast.11, s32[64,256]{1,0:T(8,128)} %bitcast.12, s32[64]{0:T(128)} %writer_stripe_in.1, f32[3,40]{1,0:T(4,128)} %gate_half_in.1, ...), custom_call_target="tpu_custom_call" | custom-call | tf_op jit(solution)/shard_map/pallas_call | solution.py:316
  74.4 1.5 %copy.16 = f32[41,4,16,256]{3,2,1,0:T(8,128)} copy(f32[41,4,16,256]{3,2,1,0:T(8,128)S(1)} %bitcast.8) | data formatting | bytes 5373952
  76.0 1.5 %copy.17 = f32[41,64,1,256]{3,2,1,0:T(1,128)} copy(f32[41,64,1,256]{3,2,1,0:T(1,128)S(1)} %bitcast.7) | data formatting | bytes 5373952

commit v4 on v3

--- a/solution.py
+++ b/solution.py
@@ -16,16 +16,18 @@
 CT, CW, CD = 4, 16, 256
 ROWS = CT * CW
 WRITERS = 64
-CUTS = (1, 12, 23, 34, 45, 64)
+CUTS = (1, 17, 28, 39, 50, 64)
 LOG2E = 1.4426950408889634
 
 
-PARTNERS = tuple((i * 27 % 64 % 8, i * 27 % 64 // 8 % 4, i * 27 % 64 // 32) for i in range(WRITERS))
-
-
-def hops(partner):
-    z, x, _ = PARTNERS[partner]
-    return min(z, 8 - z) + min(x, 4 - x)
+NEAR = (0, 1, 7)
+SPREAD = tuple((i * 27 % 64 % 8, i * 27 % 64 // 8 % 4, i * 27 % 64 // 32) for i in range(WRITERS))
+PARTNERS = (
+    SPREAD[:1]
+    + tuple(p for p in SPREAD if p[0] in (1, 7))
+    + tuple(p for p in SPREAD[1:] if p[0] not in (1, 7))
+)
+CHAIN = 3
 
 
 def kernel(
@@ -61,6 +63,7 @@
     across_in,
     width_in,
     depth_in,
+    word,
     load_sem,
     piece_send,
     piece_recv,
@@ -73,24 +76,6 @@
     def neighbour(axis, up):
         size = lax.axis_size(axis)
         return lax.rem(lax.axis_index(axis) + (1 if up else size - 1), size)
-
-    layer = [lax.rem((gy // 2) * 2 + gz // 4 + k, 8) for k in range(8)]
-    pair, odd = [(z // 2) * 2 for z in layer], [lax.rem(z, 2) * 4 for z in layer]
-    column = [lax.rem(lax.rem(gz, 4) + k, 4) for k in range(4)]
-    core = [lax.rem(gy + k, 2) for k in range(2)]
-
-    def place(i):
-        z, x, c = PARTNERS[i]
-        return pair[z] + core[c], odd[z] + column[x]
-
-    barrier = pltpu.get_barrier_semaphore()
-    for i in sorted(range(1, WRITERS), key=hops, reverse=True):
-        a, b = place(i)
-        pl.semaphore_signal(barrier, inc=1, device_id={"gy": a, "gz": b}, device_id_type=MESH)
-    for up in (False, True):
-        pl.semaphore_signal(
-            barrier, inc=1, device_id={"gx": neighbour("gx", up)}, device_id_type=MESH
-        )
 
     def load(source, target, n):
         copy = pltpu.make_async_copy(source, target, load_sem.at[n])
@@ -117,6 +102,35 @@
     ]
     state_load = load(states, new_states, 11)
 
+    layer = [lax.rem((gy // 2) * 2 + gz // 4 + k, 8) for k in range(8)]
+    pair, odd = [(z // 2) * 2 for z in layer], [lax.rem(z, 2) * 4 for z in layer]
+    column = [lax.rem(lax.rem(gz, 4) + k, 4) for k in range(4)]
+    core = [lax.rem(gy + k, 2) for k in range(2)]
+
+    def at(partner):
+        z, x, c = partner
+        return {"gy": pair[z] + core[c], "gz": odd[z] + column[x]}
+
+    def writer(i):
+        place = at(PARTNERS[i])
+        return place["gy"] * 8 + place["gz"]
+
+    barrier = pltpu.get_barrier_semaphore()
+    greeted = [p for p in PARTNERS[1:] if p[0] in NEAR]
+    for partner in sorted(greeted, key=lambda p: -min(p[1], 4 - p[1])):
+        pl.semaphore_signal(barrier, inc=1, device_id=at(partner), device_id_type=MESH)
+    for up in (False, True):
+        pl.semaphore_signal(
+            barrier, inc=1, device_id={"gx": neighbour("gx", up)}, device_id_type=MESH
+        )
+
+    def pass_word(n):
+        for z in (1, 7):
+            pl.semaphore_signal(word.at[n], inc=1, device_id=at((z, 0, 0)), device_id_type=MESH)
+
+    def get_word(n):
+        pl.semaphore_wait(word.at[n], 2)
+
     def pieces(first, last):
         rows = held.reshape(STATES * 2 * ROWS, 128)
 
@@ -126,8 +140,7 @@
             return carry
 
         for i in range(first, last):
-            a, b = place(i)
-            chosen[i] = writer_stripe[a * 8 + b]
+            chosen[i] = writer_stripe[writer(i)]
         lax.fori_loop(first, last, one, 0)
 
     def own_piece():
@@ -138,17 +151,20 @@
 
     def send_pieces(first, last):
         for i in range(first, last):
-            a, b = place(i)
             pltpu.make_async_remote_copy(
                 src_ref=send.at[i],
                 dst_ref=stripes.at[:, me],
                 send_sem=piece_send,
                 recv_sem=piece_recv,
-                device_id={"gy": a, "gz": b},
+                device_id=at(PARTNERS[i]),
                 device_id_type=MESH,
             ).start()
 
-    def face_copies(step):
+    def inner(axis, up):
+        place = lax.axis_index(axis)
+        return place < lax.axis_size(axis) - 1 if up else place > 0
+
+    def faces(step, act):
         u = excited.at[step]
         plan = []
         for up in (False, True):
@@ -156,8 +172,8 @@
             plan.append((u.at[pl.ds(48 if up else 0, 16), :], across_in.at[step, side], "gz", up))
             plan.append((width_out.at[step, side], width_in.at[step, side], "gy", up))
             plan.append((u.at[:, pl.ds(128 if up else 0, 128)], depth_in.at[step, side], "gx", up))
-        return [
-            pltpu.make_async_remote_copy(
+        for n, (src, dst, axis, up) in enumerate(plan):
+            copy = pltpu.make_async_remote_copy(
                 src_ref=src,
                 dst_ref=dst,
                 send_sem=face_send.at[step * 6 + n],
@@ -165,8 +181,10 @@
                 device_id={axis: neighbour(axis, up)},
                 device_id_type=MESH,
             )
-            for n, (src, dst, axis, up) in enumerate(plan)
-        ]
+
+            @pl.when(inner(axis, up != (act == "receive")))
+            def _(copy=copy):
+                getattr(copy, {"start": "start", "receive": "wait_recv", "end": "wait_send"}[act])()
 
     def build_tables():
         def one(g, carry):
@@ -265,26 +283,31 @@
 
     for copy in piece_loads:
         copy.wait()
-    pieces(CUTS[0], CUTS[1])
-    pl.semaphore_wait(barrier, WRITERS + 1)
-    send_pieces(CUTS[0], CUTS[1])
-    pieces(CUTS[1], CUTS[2])
+    batches = [(n, n + 4) for n in range(CUTS[0], CUTS[1], 4)]
+    pieces(*batches[0])
+    pl.semaphore_wait(barrier, len(greeted) + 2)
+    pass_word(0)
+    for n, batch in enumerate(batches):
+        pieces(*(batches[n + 1] if n + 1 < len(batches) else CUTS[1:3]))
+        send_pieces(*batch)
+    get_word(0)
+    pass_word(1)
     for copy in table_loads:
         copy.wait()
     build_tables()
+    get_word(1)
+    pass_word(2)
     state_load.wait()
     ionic(0)
+    get_word(2)
     for step in range(STEPS):
-        faces = face_copies(step)
-        for face in faces:
-            face.start()
+        faces(step, "start")
         send_pieces(CUTS[step + 1], CUTS[step + 2])
         if step + 1 < STEPS:
             pieces(CUTS[step + 2], CUTS[step + 3])
         else:
             own_piece()
-        for face in faces:
-            face.wait_recv()
+        faces(step, "receive")
         diffuse(step)
         if step + 1 < STEPS:
             ionic(step + 1)
@@ -293,8 +316,19 @@
     pltpu.make_async_copy(sent, sent, piece_send).wait()
     pltpu.make_async_copy(sent, sent, piece_recv).wait()
     for step in range(STEPS):
-        for face in face_copies(step):
-            face.wait_send()
+        faces(step, "end")
+
+
+def put_out(new_states, stripes, new_states_out, stripes_out, sem):
+    copies = [
+        pltpu.make_async_copy(source.at[rows], target.at[rows], sem.at[2 * n + k])
+        for n, rows in enumerate((pl.ds(0, 21), pl.ds(21, 20)))
+        for k, (source, target) in enumerate(((new_states, new_states_out), (stripes, stripes_out)))
+    ]
+    for copy in copies:
+        copy.start()
+    for copy in copies:
+        copy.wait()
 
 
 def per_device(
@@ -341,6 +375,7 @@
             pltpu.VMEM((STEPS, 2, CW, CD), f32),
             pltpu.VMEM((STEPS, 2, CT, CD), f32),
             pltpu.VMEM((STEPS, 2, ROWS, 128), f32),
+            pltpu.SemaphoreType.REGULAR((CHAIN,)),
             pltpu.SemaphoreType.DMA((12,)),
             pltpu.SemaphoreType.DMA,
             pltpu.SemaphoreType.DMA,
@@ -368,6 +403,20 @@
             )
         )
     )
+    new_states, stripes = pl.pallas_call(
+        put_out,
+        out_shape=(
+            jax.ShapeDtypeStruct((STATES, ROWS, CD), f32),
+            jax.ShapeDtypeStruct((STATES, WRITERS, 2, 128), f32),
+        ),
+        in_specs=[vmem, vmem],
+        out_specs=(hbm, hbm),
+        scratch_shapes=[pltpu.SemaphoreType.DMA((4,))],
+        compiler_params=pltpu.CompilerParams(vmem_limit_bytes=1024 * 1024),
+    )(
+        pltpu.with_memory_space_constraint(new_states, pltpu.VMEM),
+        pltpu.with_memory_space_constraint(stripes, pltpu.VMEM),
+    )
     return new_states.reshape(states.shape), stripes.reshape(STATES, WRITERS, 1, CD)
 
 

time: 77.6 us -> 75.5 us (0.973)
  local copies, waits for them, and re-layouts: 3.03 us -> 0 us
    unnamed x2 -> x0, local copies, waits for them, and re-layouts: 3.03 us -> none
    pallas_call x0 -> x1, Pallas kernels: none -> 2.43 us  [per_device(): pl.pallas_call(put_out, out_shape=(jax.ShapeDtypeStruct((STATES, ROWS, CD...]
    pallas_call x1, Pallas kernels: 73.8 us -> 72 us  [per_device(): pl.pallas_call(kernel, out_shape=(pltpu.VMEM((STATES, ROWS, CD), f32), pl...]
where the time goes in v4:
time: 75.5 us; the launch traced here: 75.1 us
  Pallas kernels  74.4 us (99%)
    pallas_call x1, Pallas kernels, per_device(): pl.pallas_call(kernel, out_shape=(pltpu.VMEM((STATES, ROWS, CD), f32), pl...  72 us
    pallas_call x1, Pallas kernels, per_device(): pl.pallas_call(put_out, out_shape=(jax.ShapeDtypeStruct((STATES, ROWS, CD...  2.43 us

profile of v4, /device:TPU:1, one launch (start us, length us, event | category | flops | bytes accessed | tf_op | source)
XLA Modules:
  0.0 75.1 jit_solution(5708437804493430784)
XLA Ops:
  0.6 72.0 %shard_map.122 = (f32[41,64,256]{2,1,0:T(8,128)S(1)}, f32[41,64,2,128]{3,2,1,0:T(2,128)S(1)}) custom-call(f32[41,64,256]{2,1,0:T(8,128)} %bitcast.7, f32[41,64,256]{2,1,0:T(8,128)} %bitcast.8, s32[64,256]{1,0:T(8,128)} %bitcast.9, s32[64,256]{1,0:T(8,128)} %bitcast.10, s32[64]{0:T(128)} %writer_stripe_in.1, f32[3,40]{1,0:T(4,128)} %gate_half_in.1, ...), custom_call_target="tpu_custom_call" | custom-call | tf_op jit(solution)/shard_map/pallas_call | solution.py:350
  72.6 2.4 %shard_map.123 = (f32[41,64,256]{2,1,0:T(8,128)}, f32[41,64,2,128]{3,2,1,0:T(2,128)}) custom-call(f32[41,64,256]{2,1,0:T(8,128)S(1)} %get-tuple-element.6.new_states, f32[41,64,2,128]{3,2,1,0:T(2,128)S(1)} %get-tuple-element.7.stripes), custom_call_target="tpu_custom_call" | custom-call | tf_op jit(solution)/shard_map/pallas_call | solution.py:406

commit v5 on v4

--- a/solution.py
+++ b/solution.py
@@ -16,18 +16,33 @@
 CT, CW, CD = 4, 16, 256
 ROWS = CT * CW
 WRITERS = 64
-CUTS = (1, 17, 28, 39, 50, 64)
+CUTS = (1, 18, 26, 32, 36, 42, 46, 52, 56, 64, 64)
 LOG2E = 1.4426950408889634
 
 
-NEAR = (0, 1, 7)
 SPREAD = tuple((i * 27 % 64 % 8, i * 27 % 64 // 8 % 4, i * 27 % 64 // 32) for i in range(WRITERS))
+
+
+def steps_away(partner):
+    z, x, _ = partner
+    return min(z, 8 - z) + min(x, 4 - x)
+
+
+GREETED = tuple(
+    sorted((p for p in SPREAD[1:] if steps_away(p) < 2), key=lambda p: -min(p[0], 8 - p[0]))
+)
+SECOND = tuple(p for p in SPREAD if p[0] in (1, 7) and p[1] in (1, 3))
+THIRD = tuple(
+    p for p in SPREAD[1:] if p not in GREETED + SECOND and p[0] and steps_away(p) < 5
+)[:8]
 PARTNERS = (
     SPREAD[:1]
-    + tuple(p for p in SPREAD if p[0] in (1, 7))
-    + tuple(p for p in SPREAD[1:] if p[0] not in (1, 7))
+    + GREETED
+    + SECOND
+    + THIRD
+    + tuple(p for p in SPREAD[1:] if p not in GREETED + SECOND + THIRD)
 )
-CHAIN = 3
+CHAIN = 5
 
 
 def kernel(
@@ -116,20 +131,23 @@
         return place["gy"] * 8 + place["gz"]
 
     barrier = pltpu.get_barrier_semaphore()
-    greeted = [p for p in PARTNERS[1:] if p[0] in NEAR]
-    for partner in sorted(greeted, key=lambda p: -min(p[1], 4 - p[1])):
+    for partner in GREETED:
         pl.semaphore_signal(barrier, inc=1, device_id=at(partner), device_id_type=MESH)
     for up in (False, True):
         pl.semaphore_signal(
             barrier, inc=1, device_id={"gx": neighbour("gx", up)}, device_id_type=MESH
         )
 
+    beside = ((1, 0, 0), (7, 0, 0), (0, 1, 0), (0, 3, 0))
+
     def pass_word(n):
-        for z in (1, 7):
-            pl.semaphore_signal(word.at[n], inc=1, device_id=at((z, 0, 0)), device_id_type=MESH)
+        for partner in beside:
+            pl.semaphore_signal(word.at[n], inc=1, device_id=at(partner), device_id_type=MESH)
 
     def get_word(n):
-        pl.semaphore_wait(word.at[n], 2)
+        pl.semaphore_wait(word.at[n], len(beside))
+        if n + 1 < CHAIN:
+            pass_word(n + 1)
 
     def pieces(first, last):
         rows = held.reshape(STATES * 2 * ROWS, 128)
@@ -216,6 +234,8 @@
 
     def ionic(step):
         for part in range(2):
+            if step == 0 and part == 1:
+                get_word(3)
             at = pl.ds(part * 32, 32)
             voltage = new_states[0, at, :]
 
@@ -283,40 +303,46 @@
 
     for copy in piece_loads:
         copy.wait()
-    batches = [(n, n + 4) for n in range(CUTS[0], CUTS[1], 4)]
-    pieces(*batches[0])
-    pl.semaphore_wait(barrier, len(greeted) + 2)
+    near = 1 + len(GREETED)
+    pieces(CUTS[0], near)
+    pl.semaphore_wait(barrier, len(GREETED) + 2)
     pass_word(0)
-    for n, batch in enumerate(batches):
-        pieces(*(batches[n + 1] if n + 1 < len(batches) else CUTS[1:3]))
-        send_pieces(*batch)
+    pieces(near, near + 4)
+    send_pieces(CUTS[0], near)
+    pieces(near + 4, CUTS[1])
     get_word(0)
-    pass_word(1)
+    send_pieces(near, near + 4)
+    pieces(CUTS[1], CUTS[2])
+    send_pieces(near + 4, CUTS[1])
+    get_word(1)
     for copy in table_loads:
         copy.wait()
     build_tables()
-    get_word(1)
-    pass_word(2)
+    get_word(2)
+    send_pieces(CUTS[1], CUTS[2])
+    pieces(CUTS[2], CUTS[3])
     state_load.wait()
     ionic(0)
-    get_word(2)
+    get_word(4)
     for step in range(STEPS):
         faces(step, "start")
-        send_pieces(CUTS[step + 1], CUTS[step + 2])
+        now, half, later = CUTS[2 + 2 * step : 5 + 2 * step]
+        send_pieces(now, half)
         if step + 1 < STEPS:
-            pieces(CUTS[step + 2], CUTS[step + 3])
+            pieces(half, CUTS[5 + 2 * step])
         else:
             own_piece()
         faces(step, "receive")
         diffuse(step)
+        send_pieces(half, later)
         if step + 1 < STEPS:
             ionic(step + 1)
 
+    for step in range(STEPS):
+        faces(step, "end")
     sent = send.at[pl.ds(1, WRITERS - 1)]
     pltpu.make_async_copy(sent, sent, piece_send).wait()
     pltpu.make_async_copy(sent, sent, piece_recv).wait()
-    for step in range(STEPS):
-        faces(step, "end")
 
 
 def put_out(new_states, stripes, new_states_out, stripes_out, sem):

time: 75.5 us -> 75 us (level)
  no operation moved by 1% of the time
where the time goes in v5:
time: 75 us; the launch traced here: 74.6 us
  Pallas kernels  74 us (99%)
    pallas_call x1, Pallas kernels, per_device(): pl.pallas_call(kernel, out_shape=(pltpu.VMEM((STATES, ROWS, CD), f32), pl...  71.6 us
    pallas_call x1, Pallas kernels, per_device(): pl.pallas_call(put_out, out_shape=(jax.ShapeDtypeStruct((STATES, ROWS, CD...  2.43 us

profile of v5, /device:TPU:1, one launch (start us, length us, event | category | flops | bytes accessed | tf_op | source)
XLA Modules:
  0.0 74.6 jit_solution(2652594631063651779)
XLA Ops:
  0.6 71.6 %shard_map.122 = (f32[41,64,256]{2,1,0:T(8,128)S(1)}, f32[41,64,2,128]{3,2,1,0:T(2,128)S(1)}) custom-call(f32[41,64,256]{2,1,0:T(8,128)} %bitcast.7, f32[41,64,256]{2,1,0:T(8,128)} %bitcast.8, s32[64,256]{1,0:T(8,128)} %bitcast.9, s32[64,256]{1,0:T(8,128)} %bitcast.10, s32[64]{0:T(128)} %writer_stripe_in.1, f32[3,40]{1,0:T(4,128)} %gate_half_in.1, ...), custom_call_target="tpu_custom_call" | custom-call | tf_op jit(solution)/shard_map/pallas_call | solution.py:376
  72.2 2.4 %shard_map.123 = (f32[41,64,256]{2,1,0:T(8,128)}, f32[41,64,2,128]{3,2,1,0:T(2,128)}) custom-call(f32[41,64,256]{2,1,0:T(8,128)S(1)} %get-tuple-element.6.new_states, f32[41,64,2,128]{3,2,1,0:T(2,128)S(1)} %get-tuple-element.7.stripes), custom_call_target="tpu_custom_call" | custom-call | tf_op jit(solution)/shard_map/pallas_call | solution.py:432
